TPU v7x, 8 devices: a whole 2x2x1 slice. The times are simulated.
8 devices in a mesh: dp: 4 (over z, y, x), tp: 2 (over core).
Axes of the slice: x: 2, y: 2, z: 1, core: 2. Of those that a mesh axis runs over, the one named last changes fastest.
Arguments:
- grad_qkv: bfloat16 [4, 1024, 4096], P('dp', None, 'tp')
- grad_o: bfloat16 [4, 2048, 1024], P('dp', 'tp')
- grad_gate: bfloat16 [4, 1024, 3072], P('dp', None, 'tp')
- grad_up: bfloat16 [4, 1024, 3072], P('dp', None, 'tp')
- grad_down: bfloat16 [4, 3072, 1024], P('dp', 'tp')
- w_qkv: float32 [1024, 4096], P(None, 'tp')
- w_o: float32 [2048, 1024], P('tp')
- w_gate: float32 [1024, 3072], P(None, 'tp')
- w_up: float32 [1024, 3072], P(None, 'tp')
- w_down: float32 [3072, 1024], P('tp')
- mom_qkv: float32 [1024, 4096], P(None, 'tp')
- mom_o: float32 [2048, 1024], P('tp')
- mom_gate: float32 [1024, 3072], P(None, 'tp')
- mom_up: float32 [1024, 3072], P(None, 'tp')
- mom_down: float32 [3072, 1024], P('tp')
Outputs:
- output 1: float32 [1024, 4096], P(None, 'tp')
- output 2: float32 [2048, 1024], P('tp')
- output 3: float32 [1024, 3072], P(None, 'tp')
- output 4: float32 [1024, 3072], P(None, 'tp')
- output 5: float32 [3072, 1024], P('tp')
- output 6: float32 [1024, 4096], P(None, 'tp')
- output 7: float32 [2048, 1024], P('tp')
- output 8: float32 [1024, 3072], P(None, 'tp')
- output 9: float32 [1024, 3072], P(None, 'tp')
- output 10: float32 [3072, 1024], P('tp')
All inputs are finite; a program needn't handle non-finite values.
Results may differ from a plain program's by a relative error of at most 0.02.
Values sent between devices are 32-bit elements.
A program may use at most 1 GiB of HBM per device.

v0:
```python
import math
import jax
import jax.numpy as jnp
from jax import lax
from jax.sharding import PartitionSpec as P

HEAD_DIM = 128
NEWTON_STEPS = 5
COEFF_A = 3.4445
COEFF_B = -4.7750
COEFF_C = 2.0315
MOMENTUM = 0.95
LEARN_RATE = 2e-3
WEIGHT_DECAY = 0.1
EPSILON = 1e-7
ROWS_FIRST = (False, False, False, True, False, False, True)


def gram_of(x_mat, rows_first):
    axis_k = 0 if rows_first else 1
    return lax.dot_general(x_mat, x_mat, (((axis_k,), (axis_k,)), ((), ())), preferred_element_type=jnp.float32)


def poly_times(poly_mat, x_mat, rows_first):
    if rows_first:
        return lax.dot_general(x_mat, poly_mat, (((1,), (1,)), ((), ())), preferred_element_type=jnp.float32)
    return jnp.dot(poly_mat, x_mat, preferred_element_type=jnp.float32)


def momentum_terms(grad_avgs, moms):
    mom_news = [MOMENTUM * mom_in + grad_avg for mom_in, grad_avg in zip(moms, grad_avgs)]
    nests = [grad_avg + MOMENTUM * mom_new for grad_avg, mom_new in zip(grad_avgs, mom_news)]
    return mom_news, nests


def orthogonal_updates(nests, head_count, kv_count, tp_count, tp_sum):
    nest_qkv = nests[0]
    d_model = nest_qkv.shape[0]
    group_size = head_count // kv_count
    nest_split = nest_qkv.reshape(d_model, kv_count, group_size + 2, HEAD_DIM)
    matrices = [nest_split[:, :, :group_size, :].reshape(d_model, head_count * HEAD_DIM),
                nest_split[:, :, group_size, :].reshape(d_model, kv_count * HEAD_DIM),
                nest_split[:, :, group_size + 1, :].reshape(d_model, kv_count * HEAD_DIM)] + list(nests[1:])
    squares = jnp.stack([jnp.sum(mat_item * mat_item) for mat_item in matrices])
    norm_vals = jnp.sqrt(tp_sum(squares))
    iterates = [(mat_item / (norm_vals[mat_index] + EPSILON)).astype(jnp.bfloat16) for mat_index, mat_item in enumerate(matrices)]
    for step_index in range(NEWTON_STEPS):
        gram_stack = jnp.stack([gram_of(x_mat, rows_first) for x_mat, rows_first in zip(iterates, ROWS_FIRST)])
        gram_stack = tp_sum(gram_stack)
        gram_half = gram_stack.astype(jnp.bfloat16)
        poly_stack = COEFF_B * gram_stack + COEFF_C * jnp.einsum('mde,mef->mdf', gram_half, gram_half, preferred_element_type=jnp.float32)
        poly_stack = poly_stack.astype(jnp.bfloat16)
        iterates = [(COEFF_A * x_mat.astype(jnp.float32) + poly_times(poly_stack[mat_index], x_mat, rows_first)).astype(jnp.bfloat16) for mat_index, (x_mat, rows_first) in enumerate(zip(iterates, ROWS_FIRST))]
    scaled = []
    for x_mat, rows_first in zip(iterates, ROWS_FIRST):
        long_side = (x_mat.shape[0] if rows_first else x_mat.shape[1]) * tp_count
        scaled.append(0.2 * math.sqrt(max(d_model, long_side)) * x_mat.astype(jnp.float32))
    upd_qkv = jnp.concatenate([scaled[0].reshape(d_model, kv_count, group_size, HEAD_DIM),
                               scaled[1].reshape(d_model, kv_count, 1, HEAD_DIM),
                               scaled[2].reshape(d_model, kv_count, 1, HEAD_DIM)], axis=2).reshape(d_model, -1)
    return [upd_qkv] + scaled[3:]


def apply_updates(weights, updates):
    return [weight - LEARN_RATE * (update + WEIGHT_DECAY * weight) for weight, update in zip(weights, updates)]


def solution(mesh):
    dp_count = mesh.shape['dp']
    tp_count = mesh.shape['tp']
    col_spec = P(None, 'tp')
    row_spec = P('tp', None)
    grad_col = P('dp', None, 'tp')
    grad_row = P('dp', 'tp', None)
    weight_specs = (col_spec, row_spec, col_spec, col_spec, row_spec)
    in_specs = (grad_col, grad_row, grad_col, grad_col, grad_row) + weight_specs + weight_specs
    out_specs = weight_specs + weight_specs

    def local_step(*arrays):
        grads = arrays[:5]
        weights = arrays[5:10]
        moms = arrays[10:]
        summed = lax.psum(tuple(grad_block[0].astype(jnp.float32) for grad_block in grads), 'dp')
        grad_avgs = [total_sum / dp_count for total_sum in summed]
        mom_news, nests = momentum_terms(grad_avgs, moms)
        head_count = weights[1].shape[0] // HEAD_DIM
        kv_count = (weights[0].shape[1] // HEAD_DIM - head_count) // 2
        updates = orthogonal_updates(nests, head_count, kv_count, tp_count, lambda part_sum: lax.psum(part_sum, 'tp'))
        return tuple(apply_updates(weights, updates)) + tuple(mom_news)

    return jax.shard_map(local_step, mesh=mesh, in_specs=in_specs, out_specs=out_specs, check_vma=False)
```

profile of v0, /device:TPU:0, one launch (start us, length us, event | category | flops | bytes accessed | tf_op | source)
XLA Modules:
  0.0 1597.4 jit_solution(4754946523524064908)
XLA Ops:
  12.6 6.4 copy.39
  19.0 6.8 bitcast_convert_fusion
  36.6 5.4 copy.45
  42.0 9.2 copy.40
  51.2 519.8 %all-reduce.18.cloned.1.call-done = (f32[1024,2048]{0,1:T(8,128)}, f32[1024,1024]{0,1:T(8,128)}, f32[1024,1536]{1,0:T(8,128)}, f32[1024,1536]{1,0:T(8,128)}, f32[1536,1024]{1,0:T(8,128)}) async-done(((f32[1024,2048]{0,1:T(8,128)}, f32[1024,1024]{0,1:T(8,128)}, f32[1024,1536]{1,0:T(8,128)}, f32[1024,1536]{1,0:T(8,128)}, f32[1536,1024]{1,0:T(8,128)}), (f32[1024,2048]{0,1:T(8,128)}, f32[1024,1024]{0,1:T(8,128)}, ...) | async-done | bytes 31457296 | tf_op jit(solution)/shard_map/psum | solution.py:83
  571.0 9.4 multiply_add_fusion.1
  585.1 5.3 copy.72
  602.9 7.8 multiply_add_fusion.9
  610.8 8.0 multiply_reduce_fusion.2
  618.8 7.8 multiply_reduce_fusion.1
  626.6 7.8 multiply_reduce_fusion
  646.6 6.0 divide_convert_fusion.3
  679.9 6.8 divide_convert_fusion.1
  714.3 5.3 copy.46
  719.7 57.4 %all-reduce.8.cloned.1.call-done = f32[7,1024,1024]{2,1,0:T(8,128)} async-done(((f32[7,1024,1024]{2,1,0:T(8,128)}), f32[7,1024,1024]{2,1,0:T(8,128)}) %all-reduce.8.cloned.1.call-update) | async-done | bytes 29360144 | tf_op jit(solution)/shard_map/psum | solution.py:88
  777.1 39.9 %add_convert_fusion.4 = bf16[7,1024,1024]{2,1,0:T(8,128)(2,1)S(1)} fusion(f32[7,1024,1024]{2,1,0:T(8,128)} %all-reduce.8.cloned.1.call-done), kind=kOutput, calls=%fused_computation.4 | convolution fusion | flops 15069085696 | bytes 44040192 | tf_op jit(solution)/shard_map/mde,mef->mdf/dot_general | solution.py:51
  854.6 5.0 bitcast_dynamic-update-slice_fusion.24
  864.6 5.1 bitcast_dynamic-update-slice_fusion.22
  869.8 76.5 %all-reduce.10.cloned.1.call-done = f32[7,1024,1024]{2,1,0:T(8,128)} async-done(((f32[7,1024,1024]{2,1,0:T(8,128)}), f32[7,1024,1024]{2,1,0:T(8,128)}) %all-reduce.10.cloned.1.call-update) | async-done | bytes 29360144 | tf_op jit(solution)/shard_map/psum | solution.py:88
  946.3 42.5 %add_convert_fusion.3 = bf16[7,1024,1024]{2,1,0:T(8,128)(2,1)} fusion(f32[7,1024,1024]{2,1,0:T(8,128)} %all-reduce.10.cloned.1.call-done), kind=kOutput, calls=%fused_computation.3 | convolution fusion | flops 15069085696 | bytes 44040192 | tf_op jit(solution)/shard_map/mde,mef->mdf/dot_general | solution.py:51
  988.9 5.5 add_convert_fusion.14
  994.4 6.4 add_convert_fusion.15
  1028.0 5.2 bitcast_dynamic-update-slice_fusion.17
  1038.2 5.0 bitcast_dynamic-update-slice_fusion.15
  1043.3 76.5 %all-reduce.12.cloned.1.call-done = f32[7,1024,1024]{2,1,0:T(8,128)} async-done(((f32[7,1024,1024]{2,1,0:T(8,128)}), f32[7,1024,1024]{2,1,0:T(8,128)}) %all-reduce.12.cloned.1.call-update) | async-done | bytes 29360144 | tf_op jit(solution)/shard_map/psum | solution.py:88
  1119.8 43.5 %add_convert_fusion.2 = bf16[7,1024,1024]{2,1,0:T(8,128)(2,1)} fusion(f32[7,1024,1024]{2,1,0:T(8,128)} %all-reduce.12.cloned.1.call-done), kind=kOutput, calls=%fused_computation.2 | convolution fusion | flops 15069085696 | bytes 44040192 | tf_op jit(solution)/shard_map/mde,mef->mdf/dot_general | solution.py:51
  1163.3 5.5 add_convert_fusion.11
  1168.8 6.4 add_convert_fusion.12
  1202.3 5.4 bitcast_dynamic-update-slice_fusion.10
  1212.7 5.0 bitcast_dynamic-update-slice_fusion.8
  1217.8 76.4 %all-reduce.14.cloned.1.call-done = f32[7,1024,1024]{2,1,0:T(8,128)} async-done(((f32[7,1024,1024]{2,1,0:T(8,128)}), f32[7,1024,1024]{2,1,0:T(8,128)}) %all-reduce.14.cloned.1.call-update) | async-done | bytes 29360144 | tf_op jit(solution)/shard_map/psum | solution.py:88
  1294.2 43.5 %add_convert_fusion.1 = bf16[7,1024,1024]{2,1,0:T(8,128)(2,1)} fusion(f32[7,1024,1024]{2,1,0:T(8,128)} %all-reduce.14.cloned.1.call-done), kind=kOutput, calls=%fused_computation.1 | convolution fusion | flops 15069085696 | bytes 44040192 | tf_op jit(solution)/shard_map/mde,mef->mdf/dot_general | solution.py:51
  1337.8 5.5 add_convert_fusion.8
  1343.3 6.4 add_convert_fusion.9
  1349.8 7.3 add_convert_fusion.10
  1380.2 5.2 bitcast_dynamic-update-slice_fusion.3
  1395.5 5.3 copy.61
  1400.8 5.3 copy.64
  1406.1 9.1 copy.63
  1415.3 56.7 %all-reduce.16.cloned.1.call-done = f32[7,1024,1024]{2,1,0:T(8,128)} async-done(((f32[7,1024,1024]{2,1,0:T(8,128)}), f32[7,1024,1024]{2,1,0:T(8,128)}) %all-reduce.16.cloned.1.call-update) | async-done | bytes 29360144 | tf_op jit(solution)/shard_map/psum | solution.py:88
  1472.0 39.9 %add_convert_fusion = bf16[7,1024,1024]{2,1,0:T(8,128)(2,1)S(1)} fusion(f32[7,1024,1024]{2,1,0:T(8,128)} %all-reduce.16.cloned.1.call-done), kind=kOutput, calls=%fused_computation | convolution fusion | flops 15069085696 | bytes 44040192 | tf_op jit(solution)/shard_map/mde,mef->mdf/dot_general | solution.py:51
  1527.7 5.5 copy.62
  1533.1 5.8 pad_maximum_fusion
  1539.0 9.4 copy.71
  1548.3 12.5 multiply_subtract_fusion.1
  1560.9 8.3 multiply_subtract_fusion.2
  1569.2 8.7 multiply_subtract_fusion.3
  1577.9 12.2 multiply_subtract_fusion
  (292 shorter events, 251.5 us)
Async XLA Ops:
  7.2 563.9 %all-reduce.18.cloned.1.call-start = ((), (), s32[]{:S(2)}) async-start(), calls=%async_computation.5 | async-start | bytes 62914560 | tf_op jit(solution)/shard_map/psum | solution.py:83
  36.4 740.7 %all-reduce.8.cloned.1.call-start = ((), (), s32[]{:S(2)}) async-start(), calls=%async_computation | async-start | bytes 58720256 | tf_op jit(solution)/shard_map/psum | solution.py:88
  602.9 15.8 slice-start.14
  610.8 8.0 slice-start.15
  610.8 15.8 slice-start.2
  654.3 17.6 %copy-start.6 = (bf16[1024,4,1,128]{3,0,1,2:T(8,128)(2,1)}, bf16[1024,4,1,128]{3,0,1,2:T(8,128)(2,1)S(1)}, u32[]{:S(2)}) copy-start(bf16[1024,4,1,128]{3,0,1,2:T(8,128)(2,1)S(1)} %get-tuple-element.40) | copy-start | bytes 3145732
  655.9 12.7 copy-start.8
  668.6 11.3 slice-start.12
  671.9 7.9 slice-start.8
  671.9 7.9 slice-start.13
  701.7 244.5 %all-reduce.10.cloned.1.call-start = ((), (), s32[]{:S(2)}) async-start(), calls=%async_computation.1 | async-start | bytes 58720256 | tf_op jit(solution)/shard_map/psum | solution.py:88
  719.7 97.3 %copy-start.17 = (bf16[1536,1024]{1,0:T(8,128)(2,1)S(1)}, bf16[1536,1024]{1,0:T(8,128)(2,1)}, u32[]{:S(2)}) copy-start(bf16[1536,1024]{1,0:T(8,128)(2,1)} %divide_convert_fusion) | copy-start | bytes 9437188
  821.0 43.7 %copy-start.27 = (bf16[1536,1024]{1,0:T(8,128)(2,1)}, bf16[1536,1024]{1,0:T(8,128)(2,1)S(1)}, u32[]{:S(2)}) copy-start(bf16[1536,1024]{1,0:T(8,128)(2,1)S(1)} %add_convert_fusion.17) | copy-start | bytes 9437188
  824.7 34.9 %copy-start.54 = (bf16[1024,1536]{1,0:T(8,128)(2,1)}, bf16[1024,1536]{1,0:T(8,128)(2,1)S(1)}, u32[]{:S(2)}) copy-start(bf16[1024,1536]{1,0:T(8,128)(2,1)S(1)} %add_convert_fusion.18) | copy-start | bytes 9437188
  828.6 26.0 %copy-start.56 = (bf16[1024,1536]{1,0:T(8,128)(2,1)}, bf16[1024,1536]{1,0:T(8,128)(2,1)S(1)}, u32[]{:S(2)}) copy-start(bf16[1024,1536]{1,0:T(8,128)(2,1)S(1)} %add_convert_fusion.19) | copy-start | bytes 9437188
  831.0 19.0 %copy-start.38 = (bf16[1024,1024]{0,1:T(8,128)(2,1)}, bf16[1024,1024]{0,1:T(8,128)(2,1)S(1)}, u32[]{:S(2)}) copy-start(bf16[1024,1024]{0,1:T(8,128)(2,1)S(1)} %add_convert_fusion.28) | copy-start | bytes 6291460
  869.8 250.0 %all-reduce.12.cloned.1.call-start = ((), (), s32[]{:S(2)}) async-start(), calls=%async_computation.2 | async-start | bytes 58720256 | tf_op jit(solution)/shard_map/psum | solution.py:88
  946.3 42.6 %copy-start.28 = (bf16[1536,1024]{1,0:T(8,128)(2,1)S(1)}, bf16[1536,1024]{1,0:T(8,128)(2,1)}, u32[]{:S(2)}) copy-start(bf16[1536,1024]{1,0:T(8,128)(2,1)} %copy-done.27) | copy-start | bytes 9437188
  988.8 12.0 slice-start.18
  988.8 12.0 slice-start.19
  988.8 12.0 slice-start.20
  994.3 43.8 %copy-start.29 = (bf16[1536,1024]{1,0:T(8,128)(2,1)}, bf16[1536,1024]{1,0:T(8,128)(2,1)S(1)}, u32[]{:S(2)}) copy-start(bf16[1536,1024]{1,0:T(8,128)(2,1)S(1)} %add_convert_fusion.14) | copy-start | bytes 9437188
  1000.9 32.3 %copy-start.58 = (bf16[1024,1536]{1,0:T(8,128)(2,1)}, bf16[1024,1536]{1,0:T(8,128)(2,1)S(1)}, u32[]{:S(2)}) copy-start(bf16[1024,1536]{1,0:T(8,128)(2,1)S(1)} %add_convert_fusion.15) | copy-start | bytes 9437188
  1005.0 23.1 %copy-start.60 = (bf16[1024,1536]{1,0:T(8,128)(2,1)}, bf16[1024,1536]{1,0:T(8,128)(2,1)S(1)}, u32[]{:S(2)}) copy-start(bf16[1024,1536]{1,0:T(8,128)(2,1)S(1)} %add_convert_fusion.16) | copy-start | bytes 9437188
  1007.3 16.2 %copy-start.40 = (bf16[1024,1024]{0,1:T(8,128)(2,1)}, bf16[1024,1024]{0,1:T(8,128)(2,1)S(1)}, u32[]{:S(2)}) copy-start(bf16[1024,1024]{0,1:T(8,128)(2,1)S(1)} %add_convert_fusion.26) | copy-start | bytes 6291460
  1043.3 251.0 %all-reduce.14.cloned.1.call-start = ((), (), s32[]{:S(2)}) async-start(), calls=%async_computation.3 | async-start | bytes 58720256 | tf_op jit(solution)/shard_map/psum | solution.py:88
  1119.8 43.5 %copy-start.30 = (bf16[1536,1024]{1,0:T(8,128)(2,1)S(1)}, bf16[1536,1024]{1,0:T(8,128)(2,1)}, u32[]{:S(2)}) copy-start(bf16[1536,1024]{1,0:T(8,128)(2,1)} %copy-done.29) | copy-start | bytes 9437188
  1163.3 12.0 slice-start.22
  1163.3 12.0 slice-start.23
  1163.3 12.0 slice-start.24
  1168.8 43.9 %copy-start.31 = (bf16[1536,1024]{1,0:T(8,128)(2,1)}, bf16[1536,1024]{1,0:T(8,128)(2,1)S(1)}, u32[]{:S(2)}) copy-start(bf16[1536,1024]{1,0:T(8,128)(2,1)S(1)} %add_convert_fusion.11) | copy-start | bytes 9437188
  1175.3 32.4 %copy-start.62 = (bf16[1024,1536]{1,0:T(8,128)(2,1)}, bf16[1024,1536]{1,0:T(8,128)(2,1)S(1)}, u32[]{:S(2)}) copy-start(bf16[1024,1536]{1,0:T(8,128)(2,1)S(1)} %add_convert_fusion.12) | copy-start | bytes 9437188
  1179.2 23.1 %copy-start.64 = (bf16[1024,1536]{1,0:T(8,128)(2,1)}, bf16[1024,1536]{1,0:T(8,128)(2,1)S(1)}, u32[]{:S(2)}) copy-start(bf16[1024,1536]{1,0:T(8,128)(2,1)S(1)} %add_convert_fusion.13) | copy-start | bytes 9437188
  1181.6 16.2 %copy-start.44 = (bf16[1024,1024]{0,1:T(8,128)(2,1)}, bf16[1024,1024]{0,1:T(8,128)(2,1)S(1)}, u32[]{:S(2)}) copy-start(bf16[1024,1024]{0,1:T(8,128)(2,1)S(1)} %add_convert_fusion.24) | copy-start | bytes 6291460
  1217.7 254.2 %all-reduce.16.cloned.1.call-start = ((), (), s32[]{:S(2)}) async-start(), calls=%async_computation.4 | async-start | bytes 58720256 | tf_op jit(solution)/shard_map/psum | solution.py:88
  1294.2 43.5 %copy-start.32 = (bf16[1536,1024]{1,0:T(8,128)(2,1)S(1)}, bf16[1536,1024]{1,0:T(8,128)(2,1)}, u32[]{:S(2)}) copy-start(bf16[1536,1024]{1,0:T(8,128)(2,1)} %copy-done.31) | copy-start | bytes 9437188
  1337.8 12.0 slice-start.26
  1337.8 12.0 slice-start.27
  1337.8 12.0 slice-start.28
  1343.3 47.1 %copy-start.26 = (bf16[1536,1024]{1,0:T(8,128)(2,1)}, bf16[1536,1024]{1,0:T(8,128)(2,1)S(1)}, u32[]{:S(2)}) copy-start(bf16[1536,1024]{1,0:T(8,128)(2,1)S(1)} %add_convert_fusion.8) | copy-start | bytes 9437188
  1349.8 35.6 %copy-start.50 = (bf16[1024,1536]{1,0:T(8,128)(2,1)}, bf16[1024,1536]{1,0:T(8,128)(2,1)S(1)}, u32[]{:S(2)}) copy-start(bf16[1024,1536]{1,0:T(8,128)(2,1)S(1)} %add_convert_fusion.9) | copy-start | bytes 9437188
  1357.2 23.0 %copy-start.52 = (bf16[1024,1536]{1,0:T(8,128)(2,1)}, bf16[1024,1536]{1,0:T(8,128)(2,1)S(1)}, u32[]{:S(2)}) copy-start(bf16[1024,1536]{1,0:T(8,128)(2,1)S(1)} %add_convert_fusion.10) | copy-start | bytes 9437188
  1359.5 16.2 %copy-start.36 = (bf16[1024,1024]{0,1:T(8,128)(2,1)}, bf16[1024,1024]{0,1:T(8,128)(2,1)S(1)}, u32[]{:S(2)}) copy-start(bf16[1024,1024]{0,1:T(8,128)(2,1)S(1)} %add_convert_fusion.22) | copy-start | bytes 6291460
  1511.9 10.9 copy-start.33
  1539.0 21.9 %slice-start.16 = ((s8[6291456]{0:T(1024)(128)(4,1)}), s8[2097152]{0:T(1024)(128)(4,1)S(1)}, s32[]{:S(2)}) async-start(s8[6291456]{0:T(1024)(128)(4,1)} %bitcast.410), calls=%async_computation.22 | async-start | bytes 4194304
  1548.3 12.5 slice-start.17
  1548.3 12.5 copy-start.51
  1560.9 8.3 copy-start.53
  (53 other events, 259.4 us)
Sparse Core Ops, SparseCore 0:
  36.5 534.4 all-reduce.17
  701.9 75.1 all-reduce.7
  869.9 76.3 all-reduce.9
  1043.4 76.3 all-reduce.11
  1217.9 76.3 all-reduce.13
  1395.6 76.3 all-reduce.15
where the time goes:
time: 1600 us
  waiting for transfers between devices  863 us (54%)
  matrix products  500 us (31%)
  other arithmetic  109 us (7%)
  local copies, waits for them, and re-layouts  103 us (6%)
  between operations  19.9 us (1%)
    psum x1, waiting for transfers between devices, local_step(): lax.psum(tuple((grad_block[0].astype(jnp.float32) for grad_block in grads...  520 us
    psum x5, waiting for transfers between devices, local_step(): lax.psum(part_sum, 'tp')  343 us
    dot_general x5, matrix products, orthogonal_updates(): jnp.einsum('mde,mef->mdf', gram_half, gram_half, preferred_element_type=j...  209 us
    dot_general x35, matrix products, gram_of(): lax.dot_general(x_mat, x_mat, (((axis_k,), (axis_k,)), ((), ())), preferr...  153 us
    dot_general x25, matrix products, poly_times(): return jnp.dot(poly_mat, x_mat, preferred_element_type=jnp.float32)  89.7 us
    unnamed x201, local copies, waits for them, and re-layouts  65.6 us
    dot_general x10, matrix products, poly_times(): lax.dot_general(x_mat, poly_mat, (((1,), (1,)), ((), ())), preferred_elem...  47.2 us
  transfers between devices with their start and end apart: 6, of which 6 were waited for; matrix products, arithmetic and copies ran while one was open for 3% of the time, Pallas kernels for 0%

commit v1 on v0

v1 whole, which is shorter than its diff:
```python
import functools
import math
import jax
import jax.numpy as jnp
from jax import lax
from jax.experimental import pallas as pl
from jax.experimental.pallas import tpu as pltpu
from jax.sharding import PartitionSpec as P

HEAD_DIM = 128
NEWTON_STEPS = 5
COEFF_A = 3.4445
COEFF_B = -4.7750
COEFF_C = 2.0315
MOMENTUM = 0.95
LEARN_RATE = 2e-3
WEIGHT_DECAY = 0.1
EPSILON = 1e-7
PANEL = 512
VMEM_BYTES = 67043328
F32 = jnp.float32
BF16 = jnp.bfloat16


GROUP_COLS = 2 * HEAD_DIM
MESH = pl.DeviceIdType.MESH
PIECE_R = 128
PIECE_C = 512
HALF_R = PIECE_R // 2
QUART_R = PIECE_R // 4
DOWN, GATE_UP, O_Q, KEY_VALUE = range(4)
FIRST = (0, 12, 36, 52)
LAST = (12, 36, 52, 60)
PAIRS = 60


def ds(start, size):
    return pl.ds(start if isinstance(start, int) else pl.multiple_of(start, math.gcd(size, 128)), size)


def moved_momentum(grad, mom):
    mom_new = MOMENTUM * mom + grad
    return mom_new, grad + MOMENTUM * mom_new


def weight_step(weight, x_orth, scale):
    return weight - LEARN_RATE * (scale * x_orth + WEIGHT_DECAY * weight)


def gram_panel(x_ref, depth, j):
    return lax.dot_general(x_ref[:(j + 1) * PANEL, :depth], x_ref[j * PANEL:(j + 1) * PANEL, :depth], (((1,), (1,)), ((), ())),
                           preferred_element_type=F32)


def gram_step(x_ref, depth, s_ref, sb_ref, between=lambda: None):
    for j in range(s_ref.shape[0] // PANEL):
        cols = slice(j * PANEL, (j + 1) * PANEL)
        part = gram_panel(x_ref, depth, j)
        s_ref[:(j + 1) * PANEL, cols] = part
        half = part.astype(BF16)
        sb_ref[:(j + 1) * PANEL, cols] = half
        if j:
            sb_ref[cols, :j * PANEL] = half[:j * PANEL, :].T
        between()


def poly_step(s_ref, sb_ref, t_ref, between=lambda: None):
    for j in range(s_ref.shape[0] // PANEL):
        cols = slice(j * PANEL, (j + 1) * PANEL)
        part = jnp.dot(sb_ref[:(j + 1) * PANEL, :], sb_ref[:, cols], preferred_element_type=F32)
        poly_part = (COEFF_B * s_ref[:(j + 1) * PANEL, cols] + COEFF_C * part).astype(BF16)
        t_ref[:(j + 1) * PANEL, cols] = poly_part
        if j:
            t_ref[cols, :j * PANEL] = poly_part[:j * PANEL, :].T
        between()


def advanced(t_ref, x_ref, cols):
    x_cur = x_ref[:, cols]
    prod = jnp.dot(t_ref[...], x_cur, preferred_element_type=F32)
    return (COEFF_A * x_cur.astype(F32) + prod).astype(BF16)


def step_kernel(*refs):
    (g_qkv, g_o, g_gate, g_up, g_down, w_qkv, w_o, w_gate, w_up, w_down, m_qkv, m_o, m_gate, m_up, m_down,
     wn_qkv, wn_o, wn_gate, wn_up, wn_down, mn_qkv, mn_o, mn_gate, mn_up, mn_down, kv_out,
     nbuf, xbuf, s_ref, sb_ref, t_ref, xr, wrow, wcol, snd1, half, r1, r2, fin, gbuf, mbuf, mst, nst, nst_t,
     g_sem, m_sem, ms_sem, send1, send2, send3, send4, send5, recv1, recv2, recv3, recv4, recv5,
     nsend, dsend, nrecv, xsend, xrecv, wl_sem, ws_sem, kv_sem, credit) = refs
    dp = lax.axis_index('dp')
    core = lax.axis_index('tp')
    far = 1 - core
    pos_y, pos_x = lax.div(dp, 2), lax.rem(dp, 2)
    across = (pos_y * 2 + 1 - pos_x, (1 - pos_y) * 2 + pos_x)
    place = ((pos_x, pos_y), (pos_y, pos_x))
    d = s_ref.shape[0]

    def toward(k, second):
        return {'dp': across[k ^ second]}

    barrier = pltpu.get_barrier_semaphore()
    for where in ({'dp': across[0]}, {'dp': across[1]}, {'tp': far}):
        pl.semaphore_signal(barrier, inc=1, device_id=where, device_id_type=MESH)
    pl.semaphore_wait(barrier, 3)

    def blocks(phase, k, t, mats):
        j = t - FIRST[phase]
        qkv, o, gate, up, down = mats
        if phase == DOWN:
            return [(down.at[ds(j * PIECE_R, PIECE_R), pl.ds(k * PIECE_C, PIECE_C)], slice(0, PIECE_C))]
        if phase == GATE_UP:
            return [((gate, up)[k].at[ds(lax.div(j, 3) * PIECE_R, PIECE_R), ds(lax.rem(j, 3) * PIECE_C, PIECE_C)], slice(0, PIECE_C))]
        if phase == O_Q and k == 0:
            return [(o.at[ds(lax.div(j, 2) * PIECE_R, PIECE_R), ds(lax.rem(j, 2) * PIECE_C, PIECE_C)], slice(0, PIECE_C))]
        row, part, skip = (lax.div(j, 2), lax.rem(j, 2), 0) if phase == O_Q else (j, k, GROUP_COLS)
        return [(qkv.at[ds(row * PIECE_R, PIECE_R), ds(part * 4 * GROUP_COLS + skip + 2 * g * GROUP_COLS, GROUP_COLS)],
                 slice(g * GROUP_COLS, (g + 1) * GROUP_COLS)) for g in range(2)]

    def by_phase(t, low, high, phases, fn):
        for phase in phases:
            first, last = FIRST[phase], LAST[phase]
            if high < first or low >= last:
                continue
            if low >= first and high < last:
                fn(phase)
            else:
                pl.when((t >= first) & (t < last))(functools.partial(fn, phase))

    grads = (g_qkv, g_o, g_gate, g_up, g_down)
    moms = (m_qkv, m_o, m_gate, m_up, m_down)
    mom_news = (mn_qkv, mn_o, mn_gate, mn_up, mn_down)

    def waited(ref, sem):
        pltpu.make_async_copy(ref, ref, sem).wait()

    def load_grads(t, low, high):
        def start(phase):
            for k in range(2):
                for ref, cols in blocks(phase, k, t, grads):
                    pltpu.make_async_copy(ref, gbuf.at[lax.rem(t, 8), k, :, cols], g_sem.at[lax.rem(t, 8), k]).start()
        by_phase(t, low, high, range(4), start)

    def remote(src, dst, send, recv, where):
        return pltpu.make_async_remote_copy(src_ref=src, dst_ref=dst, send_sem=send, recv_sem=recv, device_id=where,
                                            device_id_type=MESH)

    def copies(k, t, which):
        s4, s8 = lax.rem(t, 4), lax.rem(t, 8)
        a, b = place[k]
        keep = ds(a * HALF_R + b * QUART_R, QUART_R)
        got = ds(a * HALF_R + (1 - b) * QUART_R, QUART_R)
        if which == 0:
            return remote(snd1.at[s4, k], r1.at[s8, k], send1.at[s4, k], recv1.at[s8, k], toward(k, 0))
        if which == 1:
            return remote(half.at[s4, k, ds((1 - b) * QUART_R, QUART_R)], r2.at[s8, k], send2.at[s4, k], recv2.at[s8, k], toward(k, 1))
        if which == 2:
            return remote(fin.at[s8, k, keep], fin.at[s8, k, keep], send3.at[s8, k], recv3.at[s8, k], toward(k, 1))
        if which == 3:
            return remote(fin.at[s8, k, keep], fin.at[s8, k, keep], send4.at[s8, k], recv4.at[s8, k], toward(k, 0))
        return remote(fin.at[s8, k, got], fin.at[s8, k, got], send5.at[s8, k], recv5.at[s8, k], toward(k, 0))

    def send_half(t, low, high):
        s4, s8 = lax.rem(t, 4), lax.rem(t, 8)
        for k in range(2):
            waited(gbuf.at[s8, k], g_sem.at[s8, k])
            a = place[k][0]
            snd1[s4, k] = gbuf[s8, k, ds((1 - a) * HALF_R, HALF_R), :].astype(F32)
            copies(k, t, 0).start()

    def send_quarter(t, low, high):
        s4, s8 = lax.rem(t, 4), lax.rem(t, 8)
        for k in range(2):
            copies(k, t, 0).wait()
            a = place[k][0]
            half[s4, k] = gbuf[s8, k, ds(a * HALF_R, HALF_R), :].astype(F32) + r1[s8, k]
            copies(k, t, 1).start()

    def share_quarter(t, low, high):
        s4, s8 = lax.rem(t, 4), lax.rem(t, 8)
        for k in range(2):
            copies(k, t, 1).wait()
            a, b = place[k]
            fin[s8, k, ds(a * HALF_R + b * QUART_R, QUART_R), :] = (half[s4, k, ds(b * QUART_R, QUART_R), :] + r2[s8, k]) * 0.25
            copies(k, t, 2).start()
            copies(k, t, 3).start()

    def pass_quarter(t, low, high):
        s4 = lax.rem(t, 4)
        for k in range(2):
            copies(k, t, 2).wait_recv()
            copies(k, t, 4).start()

        def start(phase):
            for k in range(2):
                for ref, cols in blocks(phase, k, t, moms):
                    pltpu.make_async_copy(ref, mbuf.at[s4, k, :, cols], m_sem.at[s4, k]).start()
        by_phase(t, low, high, range(3), start)

    def away_block(t, phase, k):
        j = t - FIRST[phase]
        s2 = lax.rem(t, 2)
        if phase == GATE_UP:
            src, rows, cols = nst.at[s2], ds(lax.div(j, 3) * PIECE_R, PIECE_R), ds(lax.rem(j, 3) * PIECE_C, PIECE_C)
        elif k == 0:
            src, rows, cols = nst_t.at[s2], ds(lax.rem(j, 2) * PIECE_C, PIECE_C), ds(lax.div(j, 2) * PIECE_R, PIECE_R)
        else:
            src, rows, cols = nst.at[s2], ds(lax.div(j, 2) * PIECE_R, PIECE_R), ds(lax.rem(j, 2) * PIECE_C, PIECE_C)
        return src, rows, cols

    def retire(t, low, high):
        s2, s4, s8 = lax.rem(t, 2), lax.rem(t, 4), lax.rem(t, 8)
        for k in range(2):
            copies(k, t, 2).wait_send()
            copies(k, t, 3).wait()
            copies(k, t, 4).wait()

        def finish(phase):
            if phase == KEY_VALUE:
                for k in range(2):
                    rows = ds((t - FIRST[KEY_VALUE]) * PIECE_R, PIECE_R)
                    pltpu.make_async_copy(fin.at[s8, k], kv_out.at[rows, pl.ds(k * PIECE_C, PIECE_C)], kv_sem).start()
                return
            if phase:
                @pl.when(t == FIRST[phase])
                def _():
                    pl.semaphore_wait(credit, 1)

                @pl.when(t > FIRST[phase])
                def _():
                    waited(nst.at[lax.rem(t + 1, 2)], nsend.at[lax.rem(t + 1, 2)])
            for k in range(2):
                waited(mbuf.at[s4, k], m_sem.at[s4, k])
                if phase:
                    waited(mst.at[s4, k], ms_sem.at[s4, k])
                else:
                    @pl.when(t >= 4)
                    def _():
                        waited(mst.at[s4, k], ms_sem.at[s4, k])
                mom_new, nest = moved_momentum(fin[s8, k], mbuf[s4, k])
                mst[s4, k] = mom_new
                for ref, cols in blocks(phase, k, t, mom_news):
                    pltpu.make_async_copy(mst.at[s4, k, :, cols], ref, ms_sem.at[s4, k]).start()
                if phase == DOWN:
                    rows, cols = pl.ds(k * PIECE_C, PIECE_C), ds(t * PIECE_R, PIECE_R)
                    nbuf[core, rows, cols] = nest.T
                    remote(nbuf.at[core, rows, cols], nbuf.at[core, rows, cols], dsend, nrecv.at[DOWN], {'tp': far}).start()
                    continue
                turned = phase == O_Q and k == 0
                piece = nest.T if turned else nest
                src, rows, cols = away_block(t, phase, k)

                @pl.when(core == k)
                def _():
                    nbuf[core, rows, cols] = piece

                @pl.when(core != k)
                def _():
                    (nst_t if turned else nst)[s2] = piece
                    remote(src, nbuf.at[core, rows, cols], nsend.at[s2], nrecv.at[phase], {'tp': far}).start()
        by_phase(t, low, high, range(4), finish)

    def service(s, low, high):
        for offset, stage in ((6, pass_quarter), (4, share_quarter), (2, send_quarter), (0, send_half), (8, retire), (-2, load_grads)):
            t, lo, hi = s - offset, low - offset, high - offset
            if hi < 0 or lo >= PAIRS:
                continue
            run = functools.partial(stage, t, max(lo, 0), min(hi, PAIRS - 1))
            if lo >= 0 and hi < PAIRS:
                run()
            else:
                pl.when((t >= 0) & (t < PAIRS))(run)

    def services(low, high):
        def one(s, carry):
            service(s, low, high)
            return carry
        lax.fori_loop(low, high + 1, one, 0)

    def newton(phase, w, scale, first_service):
        waited(nbuf.at[far, :, pl.ds(0, w)], nrecv.at[phase])
        if phase == DOWN:
            waited(nbuf.at[core, :, pl.ds(0, w)], dsend)
        else:
            end = (LAST[phase] - 1) % 2
            waited(nst.at[end], nsend.at[end])
        rows_step = 64

        def square_rows(r, acc):
            rows = ds(r * rows_step, rows_step)
            a = nbuf[core, rows, :w]
            b = nbuf[far, rows, :w]
            return acc + (a * a + b * b)

        acc = lax.fori_loop(0, d // rows_step, square_rows, jnp.zeros((rows_step, w), F32))
        inv = 1.0 / (jnp.sqrt(jnp.sum(acc)) + EPSILON)

        def fill_rows(r, carry):
            rows = ds(r * rows_step, rows_step)
            xbuf[rows, :w] = (nbuf[core, rows, :w] * inv).astype(BF16)
            xbuf[rows, w:2 * w] = (nbuf[far, rows, :w] * inv).astype(BF16)
            return carry

        lax.fori_loop(0, d // rows_step, fill_rows, 0)
        if phase < O_Q:
            pl.semaphore_signal(credit, inc=1, device_id={'tp': far}, device_id_type=MESH)

        def step(i, carry):
            gram_step(xbuf, 2 * w, s_ref, sb_ref)
            last = first_service + 2 * NEWTON_STEPS - 1
            service(first_service + 2 * i, first_service, last)
            poly_step(s_ref, sb_ref, t_ref)

            @pl.when(i < NEWTON_STEPS - 1)
            def _():
                def move(c, inner):
                    cols = ds(c * PANEL, PANEL)
                    xbuf[:, cols] = advanced(t_ref, xbuf, cols)
                    return inner
                lax.fori_loop(0, 2 * w // PANEL, move, 0)
            service(first_service + 2 * i + 1, first_service, last)
            return carry

        lax.fori_loop(0, NEWTON_STEPS, step, 0)
        count = w // PANEL
        if phase != DOWN:
            def return_copy(c):
                cols = slice((c % 2) * PANEL, (c % 2 + 1) * PANEL)
                return remote(s_ref.at[:, cols], xr.at[:, pl.ds(c * PANEL, PANEL)], xsend.at[c % 2], xrecv.at[phase], {'tp': far})

            for c in range(count):
                if c >= 2:
                    return_copy(c - 2).wait_send()
                s_ref[:, (c % 2) * PANEL:(c % 2 + 1) * PANEL] = advanced(t_ref, xbuf, pl.ds(w + c * PANEL, PANEL)).astype(F32)
                return_copy(c).start()

        def own(c, carry):
            cols = ds(c * PANEL, PANEL)
            xbuf[:, cols] = advanced(t_ref, xbuf, cols)
            return carry

        lax.fori_loop(0, count, own, 0)
        if phase != DOWN:
            for c in range(max(count - 2, 0), count):
                return_copy(c).wait_send()
            waited(xr.at[:, pl.ds(0, w)], xrecv.at[phase])

        def weights(k, weight, weight_new, kind):
            buf = wrow if kind == 'rows' else wcol
            count = w // 256

            def part(ref, i):
                if kind == 'rows':
                    return ref.at[ds(i * 256, 256), :]
                return ref.at[:, ds(i * (512 if kind == 'groups' else 256), 256)]

            def load(i):
                return pltpu.make_async_copy(part(weight, i), buf.at[lax.rem(i, 3)], wl_sem.at[lax.rem(i, 3)])

            def store(i):
                return pltpu.make_async_copy(buf.at[lax.rem(i, 3)], part(weight_new, i), ws_sem.at[lax.rem(i, 3)])

            load(jnp.int32(0)).start()
            load(jnp.int32(1)).start()

            def one(i, carry):
                cols = ds(i * 256, 256)
                slot = lax.rem(i, 3)
                load(i).wait()

                def put(x_orth):
                    buf[slot] = weight_step(buf[slot], x_orth.T if kind == 'rows' else x_orth, scale)

                if phase == DOWN:
                    put(xbuf[:, cols].astype(F32))
                else:
                    @pl.when(core == k)
                    def _():
                        put(xbuf[:, cols].astype(F32))

                    @pl.when(core != k)
                    def _():
                        put(xr[:, cols])
                store(i).start()

                @pl.when(i >= 1)
                def _():
                    store(i - 1).wait()

                @pl.when(i + 2 < count)
                def _():
                    load(i + 2).start()
                return carry

            lax.fori_loop(0, count, one, 0)
            store(jnp.int32(count - 1)).wait()

        return weights

    load_grads(jnp.int32(0), 0, 0)
    load_grads(jnp.int32(1), 1, 1)
    services(0, 19)
    w_long, w_mid = w_gate.shape[1], w_o.shape[0]

    def scale_of(w):
        return 0.2 * math.sqrt(max(d, 2 * w))

    weights = newton(DOWN, w_long, scale_of(w_long), 20)
    weights(0, w_down, wn_down, 'rows')
    services(30, 43)
    weights = newton(GATE_UP, w_long, scale_of(w_long), 44)
    weights(0, w_gate, wn_gate, 'cols')
    service(jnp.int32(54), 54, 54)
    weights(1, w_up, wn_up, 'cols')
    services(55, 59)
    weights = newton(O_Q, w_mid, scale_of(w_mid), 60)
    weights(0, w_o, wn_o, 'rows')
    weights(1, w_qkv, wn_qkv, 'groups')
    for t in range(LAST[O_Q] - 4, LAST[O_Q]):
        for k in range(2):
            waited(mst.at[t % 4, k], ms_sem.at[t % 4, k])
    waited(kv_out, kv_sem)


def main_step(grads, weights, moms):
    any_spec = pl.BlockSpec(memory_space=pl.ANY)
    ins = list(grads) + list(weights) + list(moms)
    d, width = weights[0].shape
    outs = [jax.ShapeDtypeStruct(a.shape, F32) for a in list(weights) + list(moms)] + [jax.ShapeDtypeStruct((d, width // 2), F32)]
    w_long = weights[2].shape[1]
    dma = pltpu.SemaphoreType.DMA
    pieces = (PIECE_R, PIECE_C)
    return pl.pallas_call(
        step_kernel,
        out_shape=outs,
        in_specs=[any_spec] * len(ins),
        out_specs=[any_spec] * len(outs),
        scratch_shapes=[
            pltpu.VMEM((2, d, w_long), F32), pltpu.VMEM((d, 2 * w_long), BF16), pltpu.VMEM((d, d), F32), pltpu.VMEM((d, d), BF16),
            pltpu.VMEM((d, d), BF16), pltpu.VMEM((d, w_long), F32), pltpu.VMEM((3, 256, d), F32), pltpu.VMEM((3, d, 256), F32),
            pltpu.VMEM((4, 2, HALF_R, PIECE_C), F32), pltpu.VMEM((4, 2, HALF_R, PIECE_C), F32),
            pltpu.VMEM((8, 2, HALF_R, PIECE_C), F32), pltpu.VMEM((8, 2, QUART_R, PIECE_C), F32), pltpu.VMEM((8, 2) + pieces, F32),
            pltpu.VMEM((8, 2) + pieces, BF16), pltpu.VMEM((4, 2) + pieces, F32), pltpu.VMEM((4, 2) + pieces, F32),
            pltpu.VMEM((2,) + pieces, F32), pltpu.VMEM((2, PIECE_C, PIECE_R), F32),
            dma((8, 2)), dma((4, 2)), dma((4, 2)), dma((4, 2)), dma((4, 2)), dma((8, 2)), dma((8, 2)), dma((8, 2)),
            dma((8, 2)), dma((8, 2)), dma((8, 2)), dma((8, 2)), dma((8, 2)),
            dma((2,)), dma, dma((3,)), dma((2,)), dma((3,)), dma((3,)), dma((3,)), dma, pltpu.SemaphoreType.REGULAR],
        compiler_params=pltpu.CompilerParams(vmem_limit_bytes=VMEM_BYTES, collective_id=0, has_side_effects=True),
        cost_estimate=pl.CostEstimate(flops=10 ** 11, bytes_accessed=2 * 10 ** 8, transcendentals=0),
    )(*ins)


def call(body, grid, ins, in_specs, outs, out_specs, aliases=None):
    moved = sum(math.prod(a.shape) * a.dtype.itemsize for a in jax.tree.leaves((ins, outs)))
    return pl.pallas_call(
        body, grid=grid, out_shape=outs, in_specs=in_specs, out_specs=out_specs,
        input_output_aliases=aliases or {},
        compiler_params=pltpu.CompilerParams(vmem_limit_bytes=VMEM_BYTES),
        cost_estimate=pl.CostEstimate(flops=moved, bytes_accessed=moved, transcendentals=0),
    )(*ins)


def momentum_kv(grad, mom):
    rows, width = grad.shape
    odd = pl.BlockSpec((rows, GROUP_COLS), lambda g: (0, 2 * g + 1))
    block = pl.BlockSpec((rows, GROUP_COLS), lambda g: (0, g))
    head = pl.BlockSpec((rows, HEAD_DIM), lambda g: (0, g))

    def body(t_ref, m_ref, mn_ref, own_ref, away_ref):
        mn, nest = moved_momentum(t_ref[...], m_ref[...])
        mn_ref[...] = mn
        first = lax.axis_index('tp') == 0
        key, value = nest[:, :HEAD_DIM], nest[:, HEAD_DIM:]
        own_ref[...] = jnp.where(first, key, value)
        away_ref[...] = jnp.where(first, value, key)

    part = jax.ShapeDtypeStruct((rows, width // 2), F32)
    return call(body, (width // GROUP_COLS,), (grad, mom), [block, odd],
                [jax.ShapeDtypeStruct(grad.shape, F32), part, part], [block, head, head])


def update_kv(weight, x_own, x_back, weight_new, scale):
    rows, width = x_own.shape
    odd = pl.BlockSpec((rows, GROUP_COLS), lambda g: (0, 2 * g + 1))
    head = pl.BlockSpec((rows, HEAD_DIM), lambda g: (0, g))

    def body(w_ref, own_ref, back_ref, unused, o_ref):
        first = lax.axis_index('tp') == 0
        own, back = own_ref[...], back_ref[...]
        o_ref[:, :HEAD_DIM] = weight_step(w_ref[:, :HEAD_DIM], jnp.where(first, own, back), scale)
        o_ref[:, HEAD_DIM:] = weight_step(w_ref[:, HEAD_DIM:], jnp.where(first, back, own), scale)

    return call(body, (width // HEAD_DIM,), (weight, x_own, x_back, weight_new),
                [odd, head, head, pl.BlockSpec(memory_space=pl.ANY)],
                jax.ShapeDtypeStruct(weight.shape, F32), odd, {3: 0})


PARTS = 4


def finish_kernel(*refs):
    own_ref, far_ref = refs[:2]
    srcs, kv_src = refs[2:12], refs[12]
    out_own, out_far = refs[13:15]
    dsts = refs[15:25]
    x_ref, s_ref, sb_ref, t_ref = refs[25:29]
    bufs = refs[29:39]
    in_sem, out_sem = refs[39:]
    d, w = own_ref.shape
    rows_step = 128

    def fetch(n, i):
        rows = srcs[n].shape[0] // PARTS
        at = ds(i * rows, rows)
        if n != 5:
            return [pltpu.make_async_copy(srcs[n].at[at, :], bufs[n], in_sem.at[n])]
        moves = []
        for g in range(srcs[n].shape[1] // (2 * GROUP_COLS)):
            lo = 2 * g * GROUP_COLS
            moves.append(pltpu.make_async_copy(srcs[n].at[at, lo:lo + GROUP_COLS], bufs[n].at[:, lo:lo + GROUP_COLS], in_sem.at[n]))
            moves.append(pltpu.make_async_copy(kv_src.at[at, g * GROUP_COLS:(g + 1) * GROUP_COLS],
                                               bufs[n].at[:, lo + GROUP_COLS:lo + 2 * GROUP_COLS], in_sem.at[n]))
        return moves

    def put(n, i):
        rows = srcs[n].shape[0] // PARTS
        return pltpu.make_async_copy(bufs[n], dsts[n].at[ds(i * rows, rows), :], out_sem.at[n])

    def fetch_at(n, i):
        @pl.when((i > 0) & (i < PARTS))
        def _():
            put(n, i - 1).wait()

        @pl.when(i < PARTS)
        def _():
            for move in fetch(n, i):
                move.start()

    def put_at(n, i):
        @pl.when(i < PARTS)
        def _():
            pltpu.make_async_copy(bufs[n], bufs[n], in_sem.at[n]).wait()
            put(n, i).start()

    def square_rows(r, acc):
        rows = ds(r * rows_step, rows_step)
        a = own_ref[rows, :]
        b = far_ref[rows, :]
        return acc + (a * a + b * b)

    acc = lax.fori_loop(0, d // rows_step, square_rows, jnp.zeros((rows_step, w), F32))
    inv = 1.0 / (jnp.sqrt(jnp.sum(acc)) + EPSILON)

    def fill_rows(r, carry):
        rows = ds(r * rows_step, rows_step)
        x_ref[rows, :w] = (own_ref[rows, :] * inv).astype(BF16)
        x_ref[rows, w:] = (far_ref[rows, :] * inv).astype(BF16)
        return carry

    lax.fori_loop(0, d // rows_step, fill_rows, 0)

    def step(i, carry):
        order = iter(((((0, 5), ()), ((1, 6), ()), ((2, 7), (0, 5)), ((3, 8), (1, 6)), ((4, 9), (2, 7)))))

        def between():
            starts, ends = next(order)
            for n in starts:
                fetch_at(n, i)
            for n in ends:
                put_at(n, i)

        between()
        gram_step(x_ref, 2 * w, s_ref, sb_ref, between)
        poly_step(s_ref, sb_ref, t_ref, between)

        @pl.when(i < NEWTON_STEPS - 1)
        def _():
            def move(c, inner):
                cols = ds(c * PANEL, PANEL)
                x_ref[:, cols] = advanced(t_ref, x_ref, cols)
                return inner
            lax.fori_loop(0, 2 * w // PANEL, move, 0)
        for n in (3, 8, 4, 9):
            put_at(n, i)
        return carry

    lax.fori_loop(0, NEWTON_STEPS, step, 0)
    for c in range(w // PANEL):
        cols = slice(c * PANEL, (c + 1) * PANEL)
        out_far[:, cols] = advanced(t_ref, x_ref, pl.ds(w + c * PANEL, PANEL)).astype(F32)
        out_own[:, cols] = advanced(t_ref, x_ref, pl.ds(c * PANEL, PANEL)).astype(F32)
    for n in range(10):
        put(n, PARTS - 1).wait()


def finish(own, far, arrays, mom_kv):
    d, w = own.shape
    any_spec = pl.BlockSpec(memory_space=pl.ANY)
    vmem = pl.BlockSpec(memory_space=pltpu.VMEM)
    dma = pltpu.SemaphoreType.DMA
    half = jax.ShapeDtypeStruct((d, w), F32)
    return pl.pallas_call(
        finish_kernel,
        out_shape=[half, half] + [jax.ShapeDtypeStruct(a.shape, F32) for a in arrays],
        in_specs=[vmem, vmem] + [any_spec] * (len(arrays) + 1),
        out_specs=[vmem, vmem] + [any_spec] * len(arrays),
        scratch_shapes=[pltpu.VMEM((d, 2 * w), BF16), pltpu.VMEM((d, d), F32), pltpu.VMEM((d, d), BF16), pltpu.VMEM((d, d), BF16)]
        + [pltpu.VMEM((a.shape[0] // PARTS, a.shape[1]), F32) for a in arrays] + [dma((10,)), dma((10,))],
        compiler_params=pltpu.CompilerParams(vmem_limit_bytes=VMEM_BYTES),
        cost_estimate=pl.CostEstimate(flops=3 * 10 ** 10, bytes_accessed=12 * 10 ** 7, transcendentals=0),
    )(own, far, *arrays, mom_kv)


def solution(mesh):
    tp_count = mesh.shape['tp']
    col_spec = P(None, 'tp')
    row_spec = P('tp', None)
    grad_col = P('dp', None, 'tp')
    grad_row = P('dp', 'tp', None)
    weight_specs = (col_spec, row_spec, col_spec, col_spec, row_spec)
    in_specs = (grad_col, grad_row, grad_col, grad_col, grad_row) + weight_specs + weight_specs
    out_specs = weight_specs + weight_specs
    swap = [(0, 1), (1, 0)]

    def local_step(*arrays):
        weights, moms = arrays[5:10], arrays[10:]
        results = main_step([block[0] for block in arrays[:5]], weights, moms)
        arrays, grad_kv = results[:10], results[10]
        mom_kv, own, away = momentum_kv(grad_kv, moms[0])
        done = finish(own, lax.ppermute(away, 'tp', swap), arrays, mom_kv)
        x_own, x_far, done = done[0], done[1], list(done[2:])
        scale = 0.2 * math.sqrt(max(own.shape[0], own.shape[1] * tp_count))
        done[0] = update_kv(weights[0], x_own, lax.ppermute(x_far, 'tp', swap), done[0], scale)
        return tuple(done)

    return jax.shard_map(local_step, mesh=mesh, in_specs=in_specs, out_specs=out_specs, check_vma=False)
```

time: 1600 us -> 631 us (0.39)
  waiting for transfers between devices: 863 us -> 7.58 us
  Pallas kernels: 0 us -> 621 us
  matrix products: 500 us -> 0 us
  other arithmetic: 109 us -> 0 us
  local copies, waits for them, and re-layouts: 103 us -> 0 us
  between operations: 19.9 us -> 0.67 us
    psum x6 -> x0, waiting for transfers between devices: 863 us -> none  [the longest x1 520 us: local_step(): lax.psum(tuple((grad_block[0].astype(jnp.float32) for grad_block in grads...]
    pallas_call x0 -> x4, Pallas kernels: none -> 621 us  [the longest x1 554 us: main_step(): pl.pallas_call(step_kernel, out_shape=outs, in_specs=[any_spec] * len(ins...]
    dot_general x75 -> x0, matrix products: 500 us -> none  [the longest x5 209 us: orthogonal_updates(): jnp.einsum('mde,mef->mdf', gram_half, gram_half, preferred_element_type=j...]
    unnamed x201 -> x0, local copies, waits for them, and re-layouts: 65.6 us -> none
    convert_element_type x8 -> x0, other arithmetic: 36.1 us -> none  [the longest x5 19.9 us: local_step(): grad_block[0].astype(jnp.float32)]
    reduce_sum x6 -> x0, other arithmetic: 31.3 us -> none  [orthogonal_updates(): squares = jnp.stack([jnp.sum(mat_item * mat_item) for mat_item in matrices])]
    add x2 -> x0, other arithmetic: 17.2 us -> none  [momentum_terms(): MOMENTUM * mom_in + grad_avg]
  transfers between devices with their start and end apart: 6 -> 2, of which waited for: 6 -> 2; matrix products, arithmetic and copies ran while one was open for 3% -> 0% of each run, Pallas kernels for 0% -> 0%
where the time goes in v1:
time: 631 us; the launch traced here: 630 us
  Pallas kernels  621 us (98%)
  waiting for transfers between devices  7.58 us (1%)
    pallas_call x1, Pallas kernels, main_step(): pl.pallas_call(step_kernel, out_shape=outs, in_specs=[any_spec] * len(ins...  554 us
    pallas_call x1, Pallas kernels, finish(): pl.pallas_call(finish_kernel, out_shape=[half, half] + [jax.ShapeDtypeStr...  54.1 us
    pallas_call x2, Pallas kernels, call(): pl.pallas_call(body, grid=grid, out_shape=outs, in_specs=in_specs, out_sp...  13.1 us
  transfers between devices with their start and end apart: 2, of which 2 were waited for; matrix products, arithmetic and copies ran while one was open for 0% of the time, Pallas kernels for 0%

profile of v1, /device:TPU:0, one launch (start us, length us, event | category | flops | bytes accessed | tf_op | source)
XLA Modules:
  0.0 630.1 jit_solution(1478737488010606822)
XLA Ops:
  0.6 553.7 %shard_map.222 = (f32[1024,2048]{1,0:T(8,128)}, f32[1024,1024]{1,0:T(8,128)}, f32[1024,1536]{1,0:T(8,128)}, f32[1024,1536]{1,0:T(8,128)}, f32[1536,1024]{1,0:T(8...) custom-call(bf16[1024,2048]{1,0:T(8,128)(2,1)} %bitcast.5, ...), custom_call_target="tpu_custom_call" | custom-call | flops 99999997952 | bytes 200000000 | tf_op jit(solution)/shard_map/pallas_call | solution.py:432
  554.4 7.2 %shard_map.223 = (f32[1024,1024]{1,0:T(8,128)}, f32[1024,512]{1,0:T(8,128)}, f32[1024,512]{1,0:T(8,128)}) custom-call(f32[1024,1024]{1,0:T(8,128)} %get-tuple-element.36.t_ref, f32[1024,2048]{1,0:T(8,128)} %m_ref.1), custom_call_target="tpu_custom_call" | custom-call | flops 20971520 | bytes 20971520 | tf_op jit(solution)/shard_map/pallas_call | solution.py:454
  561.5 0.5 collective-permute-start
  562.0 3.8 collective-permute-done.refs_1_
  565.8 54.1 %shard_map.224 = (f32[1024,512]{1,0:T(8,128)}, f32[1024,512]{1,0:T(8,128)}, f32[1024,2048]{1,0:T(8,128)}, f32[1024,1024]{1,0:T(8,128)}, f32[1024,1536]{1,0:T(8,1...) custom-call(f32[1024,512]{1,0:T(8,128)} %get-tuple-element.37.refs_0, ...), custom_call_target="tpu_custom_call" | custom-call | flops 30000001024 | bytes 120000000 | tf_op jit(solution)/shard_map/pallas_call | solution.py:601
  620.0 0.3 collective-permute-start.1
  620.3 3.8 collective-permute-done.1.back_ref
  624.1 6.0 shard_map.225
Async XLA Ops:
  561.5 4.3 collective-permute-start
  620.0 4.1 collective-permute-start.1

commit v2 on v1

--- a/solution.py
+++ b/solution.py
@@ -29,9 +29,11 @@
 HALF_R = PIECE_R // 2
 QUART_R = PIECE_R // 4
 DOWN, GATE_UP, O_Q, KEY_VALUE = range(4)
-FIRST = (0, 12, 36, 52)
-LAST = (12, 36, 52, 60)
-PAIRS = 60
+KV_DELAY = 5
+FIRST = (0, 12, 36, 52 + KV_DELAY)
+LAST = (12, 36, 52, 60 + KV_DELAY)
+PAIRS = LAST[-1]
+BLOCK = 256
 
 
 def ds(start, size):
@@ -48,30 +50,30 @@
 
 
 def gram_panel(x_ref, depth, j):
-    return lax.dot_general(x_ref[:(j + 1) * PANEL, :depth], x_ref[j * PANEL:(j + 1) * PANEL, :depth], (((1,), (1,)), ((), ())),
+    return lax.dot_general(x_ref[:(j + 1) * BLOCK, :depth], x_ref[j * BLOCK:(j + 1) * BLOCK, :depth], (((1,), (1,)), ((), ())),
                            preferred_element_type=F32)
 
 
 def gram_step(x_ref, depth, s_ref, sb_ref, between=lambda: None):
-    for j in range(s_ref.shape[0] // PANEL):
-        cols = slice(j * PANEL, (j + 1) * PANEL)
+    for j in range(s_ref.shape[0] // BLOCK):
+        cols = slice(j * BLOCK, (j + 1) * BLOCK)
         part = gram_panel(x_ref, depth, j)
-        s_ref[:(j + 1) * PANEL, cols] = part
+        s_ref[:(j + 1) * BLOCK, cols] = part
         half = part.astype(BF16)
-        sb_ref[:(j + 1) * PANEL, cols] = half
+        sb_ref[:(j + 1) * BLOCK, cols] = half
         if j:
-            sb_ref[cols, :j * PANEL] = half[:j * PANEL, :].T
+            sb_ref[cols, :j * BLOCK] = half[:j * BLOCK, :].T
         between()
 
 
 def poly_step(s_ref, sb_ref, t_ref, between=lambda: None):
-    for j in range(s_ref.shape[0] // PANEL):
-        cols = slice(j * PANEL, (j + 1) * PANEL)
-        part = jnp.dot(sb_ref[:(j + 1) * PANEL, :], sb_ref[:, cols], preferred_element_type=F32)
-        poly_part = (COEFF_B * s_ref[:(j + 1) * PANEL, cols] + COEFF_C * part).astype(BF16)
-        t_ref[:(j + 1) * PANEL, cols] = poly_part
+    for j in range(s_ref.shape[0] // BLOCK):
+        cols = slice(j * BLOCK, (j + 1) * BLOCK)
+        part = jnp.dot(sb_ref[:(j + 1) * BLOCK, :], sb_ref[:, cols], preferred_element_type=F32)
+        poly_part = (COEFF_B * s_ref[:(j + 1) * BLOCK, cols] + COEFF_C * part).astype(BF16)
+        t_ref[:(j + 1) * BLOCK, cols] = poly_part
         if j:
-            t_ref[cols, :j * PANEL] = poly_part[:j * PANEL, :].T
+            t_ref[cols, :j * BLOCK] = poly_part[:j * BLOCK, :].T
         between()
 
 
@@ -194,7 +196,7 @@
             for k in range(2):
                 for ref, cols in blocks(phase, k, t, moms):
                     pltpu.make_async_copy(ref, mbuf.at[s4, k, :, cols], m_sem.at[s4, k]).start()
-        by_phase(t, low, high, range(3), start)
+        by_phase(t, low, high, range(4), start)
 
     def away_block(t, phase, k):
         j = t - FIRST[phase]
@@ -215,11 +217,6 @@
             copies(k, t, 4).wait()
 
         def finish(phase):
-            if phase == KEY_VALUE:
-                for k in range(2):
-                    rows = ds((t - FIRST[KEY_VALUE]) * PIECE_R, PIECE_R)
-                    pltpu.make_async_copy(fin.at[s8, k], kv_out.at[rows, pl.ds(k * PIECE_C, PIECE_C)], kv_sem).start()
-                return
             if phase:
                 @pl.when(t == FIRST[phase])
                 def _():
@@ -245,6 +242,20 @@
                     nbuf[core, rows, cols] = nest.T
                     remote(nbuf.at[core, rows, cols], nbuf.at[core, rows, cols], dsend, nrecv.at[DOWN], {'tp': far}).start()
                     continue
+                if phase == KEY_VALUE:
+                    rows = ds((t - FIRST[KEY_VALUE]) * PIECE_R, PIECE_R)
+
+                    def split(mine, nest=nest, k=k):
+                        for g in range(2):
+                            cols = slice((2 * k + g) * HEAD_DIM, (2 * k + g + 1) * HEAD_DIM)
+                            heads = [nest[:, (2 * g + h) * HEAD_DIM:(2 * g + h + 1) * HEAD_DIM] for h in range(2)]
+                            nbuf[core, rows, cols] = heads[mine]
+                            nst[s2, :, cols] = heads[1 - mine]
+                    pl.when(core == 0)(functools.partial(split, 0))
+                    pl.when(core == 1)(functools.partial(split, 1))
+                    if k:
+                        remote(nst.at[s2], nbuf.at[core, rows, pl.ds(0, 2 * GROUP_COLS)], nsend.at[s2], nrecv.at[phase], {'tp': far}).start()
+                    continue
                 turned = phase == O_Q and k == 0
                 piece = nest.T if turned else nest
                 src, rows, cols = away_block(t, phase, k)
@@ -265,10 +276,19 @@
             if hi < 0 or lo >= PAIRS:
                 continue
             run = functools.partial(stage, t, max(lo, 0), min(hi, PAIRS - 1))
-            if lo >= 0 and hi < PAIRS:
+            guards = []
+            if lo < 0:
+                guards.append(t >= 0)
+            if hi >= PAIRS:
+                guards.append(t < PAIRS)
+            if KV_DELAY and lo < FIRST[KEY_VALUE] and hi >= LAST[O_Q]:
+                if lo >= LAST[O_Q] and hi < FIRST[KEY_VALUE]:
+                    continue
+                guards.append((t - LAST[O_Q]) * (t - FIRST[KEY_VALUE] + 1) > 0)
+            if guards:
+                pl.when(functools.reduce(jnp.logical_and, guards))(run)
+            else:
                 run()
-            else:
-                pl.when((t >= 0) & (t < PAIRS))(run)
 
     def services(low, high):
         def one(s, carry):
@@ -276,7 +296,7 @@
             return carry
         lax.fori_loop(low, high + 1, one, 0)
 
-    def newton(phase, w, scale, first_service):
+    def normalize(phase, w, x_out):
         waited(nbuf.at[far, :, pl.ds(0, w)], nrecv.at[phase])
         if phase == DOWN:
             waited(nbuf.at[core, :, pl.ds(0, w)], dsend)
@@ -296,13 +316,15 @@
 
         def fill_rows(r, carry):
             rows = ds(r * rows_step, rows_step)
-            xbuf[rows, :w] = (nbuf[core, rows, :w] * inv).astype(BF16)
-            xbuf[rows, w:2 * w] = (nbuf[far, rows, :w] * inv).astype(BF16)
+            x_out[rows, :w] = (nbuf[core, rows, :w] * inv).astype(BF16)
+            x_out[rows, w:2 * w] = (nbuf[far, rows, :w] * inv).astype(BF16)
             return carry
 
         lax.fori_loop(0, d // rows_step, fill_rows, 0)
-        if phase < O_Q:
-            pl.semaphore_signal(credit, inc=1, device_id={'tp': far}, device_id_type=MESH)
+
+    def newton(phase, w, scale, first_service):
+        normalize(phase, w, xbuf)
+        pl.semaphore_signal(credit, inc=1, device_id={'tp': far}, device_id_type=MESH)
 
         def step(i, carry):
             gram_step(xbuf, 2 * w, s_ref, sb_ref)
@@ -414,18 +436,22 @@
     services(55, 59)
     weights = newton(O_Q, w_mid, scale_of(w_mid), 60)
     weights(0, w_o, wn_o, 'rows')
+    services(70, PAIRS + 7)
     weights(1, w_qkv, wn_qkv, 'groups')
-    for t in range(LAST[O_Q] - 4, LAST[O_Q]):
+    normalize(KEY_VALUE, 2 * GROUP_COLS, sb_ref)
+    copy = pltpu.make_async_copy(sb_ref, kv_out, kv_sem)
+    copy.start()
+    for slot in range(4):
         for k in range(2):
-            waited(mst.at[t % 4, k], ms_sem.at[t % 4, k])
-    waited(kv_out, kv_sem)
+            waited(mst.at[slot, k], ms_sem.at[slot, k])
+    copy.wait()
 
 
 def main_step(grads, weights, moms):
     any_spec = pl.BlockSpec(memory_space=pl.ANY)
     ins = list(grads) + list(weights) + list(moms)
     d, width = weights[0].shape
-    outs = [jax.ShapeDtypeStruct(a.shape, F32) for a in list(weights) + list(moms)] + [jax.ShapeDtypeStruct((d, width // 2), F32)]
+    outs = [jax.ShapeDtypeStruct(a.shape, F32) for a in list(weights) + list(moms)] + [jax.ShapeDtypeStruct((d, d), BF16)]
     w_long = weights[2].shape[1]
     dma = pltpu.SemaphoreType.DMA
     pieces = (PIECE_R, PIECE_C)
@@ -443,130 +469,88 @@
             pltpu.VMEM((2,) + pieces, F32), pltpu.VMEM((2, PIECE_C, PIECE_R), F32),
             dma((8, 2)), dma((4, 2)), dma((4, 2)), dma((4, 2)), dma((4, 2)), dma((8, 2)), dma((8, 2)), dma((8, 2)),
             dma((8, 2)), dma((8, 2)), dma((8, 2)), dma((8, 2)), dma((8, 2)),
-            dma((2,)), dma, dma((3,)), dma((2,)), dma((3,)), dma((3,)), dma((3,)), dma, pltpu.SemaphoreType.REGULAR],
+            dma((2,)), dma, dma((4,)), dma((2,)), dma((3,)), dma((3,)), dma((3,)), dma, pltpu.SemaphoreType.REGULAR],
         compiler_params=pltpu.CompilerParams(vmem_limit_bytes=VMEM_BYTES, collective_id=0, has_side_effects=True),
         cost_estimate=pl.CostEstimate(flops=10 ** 11, bytes_accessed=2 * 10 ** 8, transcendentals=0),
     )(*ins)
 
 
-def call(body, grid, ins, in_specs, outs, out_specs, aliases=None):
-    moved = sum(math.prod(a.shape) * a.dtype.itemsize for a in jax.tree.leaves((ins, outs)))
+def update_other(weight, x_back, weight_new, scale, core):
+    rows, width = x_back.shape
+    theirs = pl.BlockSpec((rows, HEAD_DIM), lambda g, c: (0, 4 * g + 3 - c[0]))
+
+    def body(c_ref, w_ref, back_ref, unused, o_ref):
+        o_ref[...] = weight_step(w_ref[...], back_ref[...], scale)
+
+    moved = 12 * rows * width
     return pl.pallas_call(
-        body, grid=grid, out_shape=outs, in_specs=in_specs, out_specs=out_specs,
-        input_output_aliases=aliases or {},
+        body, out_shape=jax.ShapeDtypeStruct(weight.shape, F32),
+        grid_spec=pltpu.PrefetchScalarGridSpec(
+            num_scalar_prefetch=1, grid=(width // HEAD_DIM,),
+            in_specs=[theirs, pl.BlockSpec((rows, HEAD_DIM), lambda g, c: (0, g)), pl.BlockSpec(memory_space=pl.ANY)],
+            out_specs=theirs),
+        input_output_aliases={3: 0},
         compiler_params=pltpu.CompilerParams(vmem_limit_bytes=VMEM_BYTES),
         cost_estimate=pl.CostEstimate(flops=moved, bytes_accessed=moved, transcendentals=0),
-    )(*ins)
-
-
-def momentum_kv(grad, mom):
-    rows, width = grad.shape
-    odd = pl.BlockSpec((rows, GROUP_COLS), lambda g: (0, 2 * g + 1))
-    block = pl.BlockSpec((rows, GROUP_COLS), lambda g: (0, g))
-    head = pl.BlockSpec((rows, HEAD_DIM), lambda g: (0, g))
-
-    def body(t_ref, m_ref, mn_ref, own_ref, away_ref):
-        mn, nest = moved_momentum(t_ref[...], m_ref[...])
-        mn_ref[...] = mn
-        first = lax.axis_index('tp') == 0
-        key, value = nest[:, :HEAD_DIM], nest[:, HEAD_DIM:]
-        own_ref[...] = jnp.where(first, key, value)
-        away_ref[...] = jnp.where(first, value, key)
-
-    part = jax.ShapeDtypeStruct((rows, width // 2), F32)
-    return call(body, (width // GROUP_COLS,), (grad, mom), [block, odd],
-                [jax.ShapeDtypeStruct(grad.shape, F32), part, part], [block, head, head])
-
-
-def update_kv(weight, x_own, x_back, weight_new, scale):
-    rows, width = x_own.shape
-    odd = pl.BlockSpec((rows, GROUP_COLS), lambda g: (0, 2 * g + 1))
-    head = pl.BlockSpec((rows, HEAD_DIM), lambda g: (0, g))
-
-    def body(w_ref, own_ref, back_ref, unused, o_ref):
-        first = lax.axis_index('tp') == 0
-        own, back = own_ref[...], back_ref[...]
-        o_ref[:, :HEAD_DIM] = weight_step(w_ref[:, :HEAD_DIM], jnp.where(first, own, back), scale)
-        o_ref[:, HEAD_DIM:] = weight_step(w_ref[:, HEAD_DIM:], jnp.where(first, back, own), scale)
-
-    return call(body, (width // HEAD_DIM,), (weight, x_own, x_back, weight_new),
-                [odd, head, head, pl.BlockSpec(memory_space=pl.ANY)],
-                jax.ShapeDtypeStruct(weight.shape, F32), odd, {3: 0})
+    )(core, weight, x_back, weight_new)
 
 
 PARTS = 4
 
 
 def finish_kernel(*refs):
-    own_ref, far_ref = refs[:2]
-    srcs, kv_src = refs[2:12], refs[12]
-    out_own, out_far = refs[13:15]
-    dsts = refs[15:25]
-    x_ref, s_ref, sb_ref, t_ref = refs[25:29]
-    bufs = refs[29:39]
-    in_sem, out_sem = refs[39:]
-    d, w = own_ref.shape
-    rows_step = 128
+    x_in, w_qkv = refs[:2]
+    srcs, out_far, dsts = refs[2:12], refs[12], refs[13:23]
+    x_ref, s_ref, sb_ref, t_ref, wk = refs[23:28]
+    bufs = refs[28:38]
+    in_sem, out_sem, wl_sem, ws_sem, x_sem = refs[38:]
+    d, w = out_far.shape
+    load = pltpu.make_async_copy(x_in, x_ref, x_sem)
+    load.start()
+    core = lax.axis_index('tp')
+    heads = [(g * HEAD_DIM, ds((4 * g + 2 + core) * HEAD_DIM, HEAD_DIM)) for g in range(w // HEAD_DIM)]
+    scale = 0.2 * math.sqrt(max(d, 2 * w))
+    for lo, at in heads:
+        pltpu.make_async_copy(w_qkv.at[:, at], wk.at[:, lo:lo + HEAD_DIM], wl_sem).start()
 
     def fetch(n, i):
         rows = srcs[n].shape[0] // PARTS
-        at = ds(i * rows, rows)
-        if n != 5:
-            return [pltpu.make_async_copy(srcs[n].at[at, :], bufs[n], in_sem.at[n])]
-        moves = []
-        for g in range(srcs[n].shape[1] // (2 * GROUP_COLS)):
-            lo = 2 * g * GROUP_COLS
-            moves.append(pltpu.make_async_copy(srcs[n].at[at, lo:lo + GROUP_COLS], bufs[n].at[:, lo:lo + GROUP_COLS], in_sem.at[n]))
-            moves.append(pltpu.make_async_copy(kv_src.at[at, g * GROUP_COLS:(g + 1) * GROUP_COLS],
-                                               bufs[n].at[:, lo + GROUP_COLS:lo + 2 * GROUP_COLS], in_sem.at[n]))
-        return moves
+        return pltpu.make_async_copy(srcs[n].at[ds(i * rows, rows), :], bufs[n], in_sem.at[n])
 
     def put(n, i):
         rows = srcs[n].shape[0] // PARTS
         return pltpu.make_async_copy(bufs[n], dsts[n].at[ds(i * rows, rows), :], out_sem.at[n])
 
     def fetch_at(n, i):
+        i = i - n // 5
+
         @pl.when((i > 0) & (i < PARTS))
         def _():
             put(n, i - 1).wait()
 
-        @pl.when(i < PARTS)
+        @pl.when((i >= 0) & (i < PARTS))
         def _():
-            for move in fetch(n, i):
-                move.start()
+            fetch(n, i).start()
 
     def put_at(n, i):
-        @pl.when(i < PARTS)
+        i = i - n // 5
+
+        @pl.when((i >= 0) & (i < PARTS))
         def _():
-            pltpu.make_async_copy(bufs[n], bufs[n], in_sem.at[n]).wait()
+            fetch(n, i).wait()
             put(n, i).start()
 
-    def square_rows(r, acc):
-        rows = ds(r * rows_step, rows_step)
-        a = own_ref[rows, :]
-        b = far_ref[rows, :]
-        return acc + (a * a + b * b)
-
-    acc = lax.fori_loop(0, d // rows_step, square_rows, jnp.zeros((rows_step, w), F32))
-    inv = 1.0 / (jnp.sqrt(jnp.sum(acc)) + EPSILON)
-
-    def fill_rows(r, carry):
-        rows = ds(r * rows_step, rows_step)
-        x_ref[rows, :w] = (own_ref[rows, :] * inv).astype(BF16)
-        x_ref[rows, w:] = (far_ref[rows, :] * inv).astype(BF16)
-        return carry
-
-    lax.fori_loop(0, d // rows_step, fill_rows, 0)
-
     def step(i, carry):
-        order = iter(((((0, 5), ()), ((1, 6), ()), ((2, 7), (0, 5)), ((3, 8), (1, 6)), ((4, 9), (2, 7)))))
+        starts = {0: (0, 5), 2: (1, 6), 4: (2, 7), 6: (3, 8), 8: (4, 9)}
+        ends = {3: (0, 5), 5: (1, 6), 7: (2, 7)}
+        slots = iter(range(9))
 
         def between():
-            starts, ends = next(order)
-            for n in starts:
+            slot = next(slots)
+            for n in ends.get(slot, ()):
+                put_at(n, i)
+            for n in starts.get(slot, ()):
                 fetch_at(n, i)
-            for n in ends:
-                put_at(n, i)
 
         between()
         gram_step(x_ref, 2 * w, s_ref, sb_ref, between)
@@ -583,31 +567,38 @@
             put_at(n, i)
         return carry
 
+    load.wait()
     lax.fori_loop(0, NEWTON_STEPS, step, 0)
     for c in range(w // PANEL):
         cols = slice(c * PANEL, (c + 1) * PANEL)
         out_far[:, cols] = advanced(t_ref, x_ref, pl.ds(w + c * PANEL, PANEL)).astype(F32)
-        out_own[:, cols] = advanced(t_ref, x_ref, pl.ds(c * PANEL, PANEL)).astype(F32)
+    pltpu.make_async_copy(wk, wk, wl_sem).wait()
+    for c in range(w // PANEL):
+        cols = slice(c * PANEL, (c + 1) * PANEL)
+        wk[:, cols] = weight_step(wk[:, cols], advanced(t_ref, x_ref, pl.ds(c * PANEL, PANEL)).astype(F32), scale)
     for n in range(10):
         put(n, PARTS - 1).wait()
-
-
-def finish(own, far, arrays, mom_kv):
-    d, w = own.shape
+    for lo, at in heads:
+        pltpu.make_async_copy(wk.at[:, lo:lo + HEAD_DIM], dsts[0].at[:, at], ws_sem).start()
+    pltpu.make_async_copy(wk, wk, ws_sem).wait()
+
+
+def finish(x_kv, w_qkv, arrays):
+    d = x_kv.shape[0]
+    w = x_kv.shape[1] // 2
     any_spec = pl.BlockSpec(memory_space=pl.ANY)
     vmem = pl.BlockSpec(memory_space=pltpu.VMEM)
     dma = pltpu.SemaphoreType.DMA
-    half = jax.ShapeDtypeStruct((d, w), F32)
     return pl.pallas_call(
         finish_kernel,
-        out_shape=[half, half] + [jax.ShapeDtypeStruct(a.shape, F32) for a in arrays],
-        in_specs=[vmem, vmem] + [any_spec] * (len(arrays) + 1),
-        out_specs=[vmem, vmem] + [any_spec] * len(arrays),
-        scratch_shapes=[pltpu.VMEM((d, 2 * w), BF16), pltpu.VMEM((d, d), F32), pltpu.VMEM((d, d), BF16), pltpu.VMEM((d, d), BF16)]
-        + [pltpu.VMEM((a.shape[0] // PARTS, a.shape[1]), F32) for a in arrays] + [dma((10,)), dma((10,))],
+        out_shape=[jax.ShapeDtypeStruct((d, w), F32)] + [jax.ShapeDtypeStruct(a.shape, F32) for a in arrays],
+        in_specs=[any_spec] * (len(arrays) + 2),
+        out_specs=[vmem] + [any_spec] * len(arrays),
+        scratch_shapes=[pltpu.VMEM((d, d), BF16), pltpu.VMEM((d, d), F32), pltpu.VMEM((d, d), BF16), pltpu.VMEM((d, d), BF16), pltpu.VMEM((d, w), F32)]
+        + [pltpu.VMEM((a.shape[0] // PARTS, a.shape[1]), F32) for a in arrays] + [dma((10,)), dma((10,)), dma, dma, dma],
         compiler_params=pltpu.CompilerParams(vmem_limit_bytes=VMEM_BYTES),
         cost_estimate=pl.CostEstimate(flops=3 * 10 ** 10, bytes_accessed=12 * 10 ** 7, transcendentals=0),
-    )(own, far, *arrays, mom_kv)
+    )(x_kv, w_qkv, *arrays)
 
 
 def solution(mesh):
@@ -624,12 +615,11 @@
     def local_step(*arrays):
         weights, moms = arrays[5:10], arrays[10:]
         results = main_step([block[0] for block in arrays[:5]], weights, moms)
-        arrays, grad_kv = results[:10], results[10]
-        mom_kv, own, away = momentum_kv(grad_kv, moms[0])
-        done = finish(own, lax.ppermute(away, 'tp', swap), arrays, mom_kv)
-        x_own, x_far, done = done[0], done[1], list(done[2:])
-        scale = 0.2 * math.sqrt(max(own.shape[0], own.shape[1] * tp_count))
-        done[0] = update_kv(weights[0], x_own, lax.ppermute(x_far, 'tp', swap), done[0], scale)
+        done = finish(results[10], weights[0], results[:10])
+        x_far, done = done[0], list(done[1:])
+        scale = 0.2 * math.sqrt(max(x_far.shape[0], x_far.shape[1] * tp_count))
+        core = lax.axis_index('tp').astype(jnp.int32).reshape(1)
+        done[0] = update_other(weights[0], lax.ppermute(x_far, 'tp', swap), done[0], scale, core)
         return tuple(done)
 
     return jax.shard_map(local_step, mesh=mesh, in_specs=in_specs, out_specs=out_specs, check_vma=False)

time: 631 us -> 631 us (level); the launches traced: 630 us -> 624 us
    pallas_call x3 -> x2, Pallas kernels: 67.3 us -> 66 us  [the longest x1 61.7 us: finish(): pl.pallas_call(finish_kernel, out_shape=[jax.ShapeDtypeStruct((d, w), F32...]
  transfers between devices with their start and end apart: 2 -> 1, of which waited for: 2 -> 1; matrix products, arithmetic and copies ran while one was open for 0% -> 0% of each run, Pallas kernels for 0% -> 0%
where the time goes in v2:
time: 631 us; the launch traced here: 624 us
  Pallas kernels  618 us (98%)
    pallas_call x1, Pallas kernels, main_step(): pl.pallas_call(step_kernel, out_shape=outs, in_specs=[any_spec] * len(ins...  552 us
    pallas_call x1, Pallas kernels, finish(): pl.pallas_call(finish_kernel, out_shape=[jax.ShapeDtypeStruct((d, w), F32...  61.7 us
  transfers between devices with their start and end apart: 1, of which 1 were waited for; matrix products, arithmetic and copies ran while one was open for 0% of the time, Pallas kernels for 0%

profile of v2, /device:TPU:0, one launch (start us, length us, event | category | flops | bytes accessed | tf_op | source)
XLA Modules:
  0.0 623.7 jit_solution(2312034782261572280)
XLA Ops:
  0.6 552.5 %shard_map.222 = (f32[1024,2048]{1,0:T(8,128)}, f32[1024,1024]{1,0:T(8,128)}, f32[1024,1536]{1,0:T(8,128)}, f32[1024,1536]{1,0:T(8,128)}, f32[1536,1024]{1,0:T(8...) custom-call(bf16[1024,2048]{1,0:T(8,128)(2,1)} %bitcast.6, ...), custom_call_target="tpu_custom_call" | custom-call | flops 99999997952 | bytes 200000000 | tf_op jit(solution)/shard_map/pallas_call | solution.py:458
  553.1 61.7 %shard_map.223 = (f32[1024,512]{1,0:T(8,128)}, f32[1024,2048]{1,0:T(8,128)}, f32[1024,1024]{1,0:T(8,128)}, f32[1024,1536]{1,0:T(8,128)}, f32[1024,1536]{1,0:T(8,...) custom-call(bf16[1024,1024]{1,0:T(8,128)(2,1)} %get-tuple-element.32, ...), custom_call_target="tpu_custom_call" | custom-call | flops 30000001024 | bytes 120000000 | tf_op jit(solution)/shard_map/pallas_call | solution.py:592
  614.8 0.0 collective-permute-start
  614.9 4.1 collective-permute-done.back_ref
  619.0 4.3 shard_map.224
Async XLA Ops:
  614.8 4.1 collective-permute-start

commit v3 on v2

--- a/solution.py
+++ b/solution.py
@@ -33,7 +33,7 @@
 FIRST = (0, 12, 36, 52 + KV_DELAY)
 LAST = (12, 36, 52, 60 + KV_DELAY)
 PAIRS = LAST[-1]
-BLOCK = 256
+BLOCK = 512
 
 
 def ds(start, size):
@@ -49,32 +49,30 @@
     return weight - LEARN_RATE * (scale * x_orth + WEIGHT_DECAY * weight)
 
 
-def gram_panel(x_ref, depth, j):
-    return lax.dot_general(x_ref[:(j + 1) * BLOCK, :depth], x_ref[j * BLOCK:(j + 1) * BLOCK, :depth], (((1,), (1,)), ((), ())),
+def gram_panel(x_ref, depth, j, block):
+    return lax.dot_general(x_ref[:(j + 1) * block, :depth], x_ref[j * block:(j + 1) * block, :depth], (((1,), (1,)), ((), ())),
                            preferred_element_type=F32)
 
 
-def gram_step(x_ref, depth, s_ref, sb_ref, between=lambda: None):
-    for j in range(s_ref.shape[0] // BLOCK):
-        cols = slice(j * BLOCK, (j + 1) * BLOCK)
-        part = gram_panel(x_ref, depth, j)
-        s_ref[:(j + 1) * BLOCK, cols] = part
+def gram_step(x_ref, depth, s_ref, sb_ref, block):
+    for j in range(s_ref.shape[0] // block):
+        cols = slice(j * block, (j + 1) * block)
+        part = gram_panel(x_ref, depth, j, block)
+        s_ref[:(j + 1) * block, cols] = part
         half = part.astype(BF16)
-        sb_ref[:(j + 1) * BLOCK, cols] = half
+        sb_ref[:(j + 1) * block, cols] = half
         if j:
-            sb_ref[cols, :j * BLOCK] = half[:j * BLOCK, :].T
-        between()
-
-
-def poly_step(s_ref, sb_ref, t_ref, between=lambda: None):
-    for j in range(s_ref.shape[0] // BLOCK):
-        cols = slice(j * BLOCK, (j + 1) * BLOCK)
-        part = jnp.dot(sb_ref[:(j + 1) * BLOCK, :], sb_ref[:, cols], preferred_element_type=F32)
-        poly_part = (COEFF_B * s_ref[:(j + 1) * BLOCK, cols] + COEFF_C * part).astype(BF16)
-        t_ref[:(j + 1) * BLOCK, cols] = poly_part
+            sb_ref[cols, :j * block] = half[:j * block, :].T
+
+
+def poly_step(s_ref, sb_ref, t_ref, block):
+    for j in range(s_ref.shape[0] // block):
+        cols = slice(j * block, (j + 1) * block)
+        part = jnp.dot(sb_ref[:(j + 1) * block, :], sb_ref[:, cols], preferred_element_type=F32)
+        poly_part = (COEFF_B * s_ref[:(j + 1) * block, cols] + COEFF_C * part).astype(BF16)
+        t_ref[:(j + 1) * block, cols] = poly_part
         if j:
-            t_ref[cols, :j * BLOCK] = poly_part[:j * BLOCK, :].T
-        between()
+            t_ref[cols, :j * block] = poly_part[:j * block, :].T
 
 
 def advanced(t_ref, x_ref, cols):
@@ -327,10 +325,11 @@
         pl.semaphore_signal(credit, inc=1, device_id={'tp': far}, device_id_type=MESH)
 
         def step(i, carry):
-            gram_step(xbuf, 2 * w, s_ref, sb_ref)
+            block = BLOCK if phase == O_Q else PANEL
+            gram_step(xbuf, 2 * w, s_ref, sb_ref, block)
             last = first_service + 2 * NEWTON_STEPS - 1
             service(first_service + 2 * i, first_service, last)
-            poly_step(s_ref, sb_ref, t_ref)
+            poly_step(s_ref, sb_ref, t_ref, block)
 
             @pl.when(i < NEWTON_STEPS - 1)
             def _():
@@ -366,7 +365,7 @@
                 return_copy(c).wait_send()
             waited(xr.at[:, pl.ds(0, w)], xrecv.at[phase])
 
-        def weights(k, weight, weight_new, kind):
+        def weights(k, weight, weight_new, kind, first=None):
             buf = wrow if kind == 'rows' else wcol
             count = w // 256
 
@@ -411,6 +410,10 @@
                 @pl.when(i + 2 < count)
                 def _():
                     load(i + 2).start()
+                if first is not None:
+                    @pl.when(lax.rem(i, 3) == 2)
+                    def _():
+                        service(first + lax.div(i, 3), first, first + 1)
                 return carry
 
             lax.fori_loop(0, count, one, 0)
@@ -427,13 +430,12 @@
         return 0.2 * math.sqrt(max(d, 2 * w))
 
     weights = newton(DOWN, w_long, scale_of(w_long), 20)
-    weights(0, w_down, wn_down, 'rows')
-    services(30, 43)
+    weights(0, w_down, wn_down, 'rows', 30)
+    services(32, 43)
     weights = newton(GATE_UP, w_long, scale_of(w_long), 44)
-    weights(0, w_gate, wn_gate, 'cols')
-    service(jnp.int32(54), 54, 54)
+    weights(0, w_gate, wn_gate, 'cols', 54)
     weights(1, w_up, wn_up, 'cols')
-    services(55, 59)
+    services(56, 59)
     weights = newton(O_Q, w_mid, scale_of(w_mid), 60)
     weights(0, w_o, wn_o, 'rows')
     services(70, PAIRS + 7)
@@ -495,15 +497,12 @@
     )(core, weight, x_back, weight_new)
 
 
-PARTS = 4
-
-
 def finish_kernel(*refs):
     x_in, w_qkv = refs[:2]
     srcs, out_far, dsts = refs[2:12], refs[12], refs[13:23]
     x_ref, s_ref, sb_ref, t_ref, wk = refs[23:28]
-    bufs = refs[28:38]
-    in_sem, out_sem, wl_sem, ws_sem, x_sem = refs[38:]
+    bufs = refs[28:34]
+    in_sem, out_sem, wl_sem, ws_sem, x_sem = refs[34:]
     d, w = out_far.shape
     load = pltpu.make_async_copy(x_in, x_ref, x_sem)
     load.start()
@@ -513,48 +512,45 @@
     for lo, at in heads:
         pltpu.make_async_copy(w_qkv.at[:, at], wk.at[:, lo:lo + HEAD_DIM], wl_sem).start()
 
-    def fetch(n, i):
-        rows = srcs[n].shape[0] // PARTS
-        return pltpu.make_async_copy(srcs[n].at[ds(i * rows, rows), :], bufs[n], in_sem.at[n])
-
-    def put(n, i):
-        rows = srcs[n].shape[0] // PARTS
-        return pltpu.make_async_copy(bufs[n], dsts[n].at[ds(i * rows, rows), :], out_sem.at[n])
-
-    def fetch_at(n, i):
-        i = i - n // 5
-
-        @pl.when((i > 0) & (i < PARTS))
-        def _():
-            put(n, i - 1).wait()
-
-        @pl.when((i >= 0) & (i < PARTS))
-        def _():
-            fetch(n, i).start()
-
-    def put_at(n, i):
-        i = i - n // 5
-
-        @pl.when((i >= 0) & (i < PARTS))
-        def _():
-            fetch(n, i).wait()
-            put(n, i).start()
+    moves = [(srcs[n], dsts[n]) for n in (4, 9, 2, 7, 3, 8)]
+    moves += [(srcs[n], dsts[n]) for n in (1, 6)]
+    moves += [(srcs[n].at[:, lo:lo + d], dsts[n].at[:, lo:lo + d]) for n in (0, 5) for lo in (0, d)]
+
+    def held(n):
+        return bufs[n] if n < 6 else bufs[n - 6].at[:d, :d]
+
+    def fetch(n):
+        if n >= 6:
+            put_copy(n - 6).wait()
+        pltpu.make_async_copy(moves[n][0], held(n), in_sem.at[n]).start()
+
+    def put_copy(n):
+        return pltpu.make_async_copy(held(n), moves[n][1], out_sem.at[n])
+
+    def put(n):
+        pltpu.make_async_copy(moves[n][0], held(n), in_sem.at[n]).wait()
+        put_copy(n).start()
+
+    for n in range(6):
+        fetch(n)
+    plan = {(0, 1): ((put, 0),), (0, 2): ((put, 1),), (1, 0): ((put, 2),), (1, 1): ((put, 3),), (1, 2): ((fetch, 6),),
+            (2, 0): ((put, 4),), (2, 1): ((put, 5), (fetch, 7)), (2, 2): ((fetch, 8),), (3, 0): ((put, 6), (fetch, 9)),
+            (3, 1): ((put, 7), (fetch, 10)), (3, 2): ((put, 8),), (4, 0): ((fetch, 11), (put, 9)), (4, 1): ((put, 10),)}
 
     def step(i, carry):
-        starts = {0: (0, 5), 2: (1, 6), 4: (2, 7), 6: (3, 8), 8: (4, 9)}
-        ends = {3: (0, 5), 5: (1, 6), 7: (2, 7)}
-        slots = iter(range(9))
-
-        def between():
-            slot = next(slots)
-            for n in ends.get(slot, ()):
-                put_at(n, i)
-            for n in starts.get(slot, ()):
-                fetch_at(n, i)
-
-        between()
-        gram_step(x_ref, 2 * w, s_ref, sb_ref, between)
-        poly_step(s_ref, sb_ref, t_ref, between)
+        def at(slot):
+            for turn in range(NEWTON_STEPS):
+                if (turn, slot) in plan:
+                    @pl.when(i == turn)
+                    def _(todo=plan[turn, slot]):
+                        for act, n in todo:
+                            act(n)
+
+        at(0)
+        gram_step(x_ref, 2 * w, s_ref, sb_ref, BLOCK)
+        at(1)
+        poly_step(s_ref, sb_ref, t_ref, BLOCK)
+        at(2)
 
         @pl.when(i < NEWTON_STEPS - 1)
         def _():
@@ -563,12 +559,11 @@
                 x_ref[:, cols] = advanced(t_ref, x_ref, cols)
                 return inner
             lax.fori_loop(0, 2 * w // PANEL, move, 0)
-        for n in (3, 8, 4, 9):
-            put_at(n, i)
         return carry
 
     load.wait()
     lax.fori_loop(0, NEWTON_STEPS, step, 0)
+    put(11)
     for c in range(w // PANEL):
         cols = slice(c * PANEL, (c + 1) * PANEL)
         out_far[:, cols] = advanced(t_ref, x_ref, pl.ds(w + c * PANEL, PANEL)).astype(F32)
@@ -576,8 +571,8 @@
     for c in range(w // PANEL):
         cols = slice(c * PANEL, (c + 1) * PANEL)
         wk[:, cols] = weight_step(wk[:, cols], advanced(t_ref, x_ref, pl.ds(c * PANEL, PANEL)).astype(F32), scale)
-    for n in range(10):
-        put(n, PARTS - 1).wait()
+    for n in range(6, 12):
+        put_copy(n).wait()
     for lo, at in heads:
         pltpu.make_async_copy(wk.at[:, lo:lo + HEAD_DIM], dsts[0].at[:, at], ws_sem).start()
     pltpu.make_async_copy(wk, wk, ws_sem).wait()
@@ -595,7 +590,7 @@
         in_specs=[any_spec] * (len(arrays) + 2),
         out_specs=[vmem] + [any_spec] * len(arrays),
         scratch_shapes=[pltpu.VMEM((d, d), BF16), pltpu.VMEM((d, d), F32), pltpu.VMEM((d, d), BF16), pltpu.VMEM((d, d), BF16), pltpu.VMEM((d, w), F32)]
-        + [pltpu.VMEM((a.shape[0] // PARTS, a.shape[1]), F32) for a in arrays] + [dma((10,)), dma((10,)), dma, dma, dma],
+        + [pltpu.VMEM(arrays[n].shape, F32) for n in (4, 9, 2, 7, 3, 8)] + [dma((12,)), dma((12,)), dma, dma, dma],
         compiler_params=pltpu.CompilerParams(vmem_limit_bytes=VMEM_BYTES),
         cost_estimate=pl.CostEstimate(flops=3 * 10 ** 10, bytes_accessed=12 * 10 ** 7, transcendentals=0),
     )(x_kv, w_qkv, *arrays)

time: 631 us -> 604 us (0.957); the launches traced: 624 us -> 604 us
  Pallas kernels: 618 us -> 599 us
    pallas_call x1, Pallas kernels: 61.7 us -> 47.2 us  [finish(): pl.pallas_call(finish_kernel, out_shape=[jax.ShapeDtypeStruct((d, w), F32...]
where the time goes in v3:
time: 604 us
  Pallas kernels  599 us (99%)
    pallas_call x1, Pallas kernels, main_step(): pl.pallas_call(step_kernel, out_shape=outs, in_specs=[any_spec] * len(ins...  547 us
    pallas_call x1, Pallas kernels, finish(): pl.pallas_call(finish_kernel, out_shape=[jax.ShapeDtypeStruct((d, w), F32...  47.2 us
  transfers between devices with their start and end apart: 1, of which 1 were waited for; matrix products, arithmetic and copies ran while one was open for 0% of the time, Pallas kernels for 0%

profile of v3, /device:TPU:0, one launch (start us, length us, event | category | flops | bytes accessed | tf_op | source)
XLA Modules:
  0.0 603.6 jit_solution(7695687118355107794)
XLA Ops:
  0.6 547.4 %shard_map.222 = (f32[1024,2048]{1,0:T(8,128)}, f32[1024,1024]{1,0:T(8,128)}, f32[1024,1536]{1,0:T(8,128)}, f32[1024,1536]{1,0:T(8,128)}, f32[1536,1024]{1,0:T(8...) custom-call(bf16[1024,2048]{1,0:T(8,128)(2,1)} %bitcast.6, ...), custom_call_target="tpu_custom_call" | custom-call | flops 99999997952 | bytes 200000000 | tf_op jit(solution)/shard_map/pallas_call | solution.py:460
  548.0 47.2 %shard_map.223 = (f32[1024,512]{1,0:T(8,128)}, f32[1024,2048]{1,0:T(8,128)}, f32[1024,1024]{1,0:T(8,128)}, f32[1024,1536]{1,0:T(8,128)}, f32[1024,1536]{1,0:T(8,...) custom-call(bf16[1024,1024]{1,0:T(8,128)(2,1)} %get-tuple-element.32, ...), custom_call_target="tpu_custom_call" | custom-call | flops 30000001024 | bytes 120000000 | tf_op jit(solution)/shard_map/pallas_call | solution.py:587
  595.2 0.0 collective-permute-start
  595.2 4.1 collective-permute-done.back_ref
  599.3 4.3 shard_map.224
Async XLA Ops:
  595.2 4.1 collective-permute-start

commit v4 on v3

--- a/solution.py
+++ b/solution.py
@@ -83,7 +83,7 @@
 
 def step_kernel(*refs):
     (g_qkv, g_o, g_gate, g_up, g_down, w_qkv, w_o, w_gate, w_up, w_down, m_qkv, m_o, m_gate, m_up, m_down,
-     wn_qkv, wn_o, wn_gate, wn_up, wn_down, mn_qkv, mn_o, mn_gate, mn_up, mn_down, kv_out,
+     wn_gate, wn_up, wn_down, mn_qkv, mn_o, mn_gate, mn_up, mn_down, kv_out, own_out, other_out,
      nbuf, xbuf, s_ref, sb_ref, t_ref, xr, wrow, wcol, snd1, half, r1, r2, fin, gbuf, mbuf, mst, nst, nst_t,
      g_sem, m_sem, ms_sem, send1, send2, send3, send4, send5, recv1, recv2, recv3, recv4, recv5,
      nsend, dsend, nrecv, xsend, xrecv, wl_sem, ws_sem, kv_sem, credit) = refs
@@ -372,7 +372,7 @@
             def part(ref, i):
                 if kind == 'rows':
                     return ref.at[ds(i * 256, 256), :]
-                return ref.at[:, ds(i * (512 if kind == 'groups' else 256), 256)]
+                return ref.at[:, ds(i * 256, 256)]
 
             def load(i):
                 return pltpu.make_async_copy(part(weight, i), buf.at[lax.rem(i, 3)], wl_sem.at[lax.rem(i, 3)])
@@ -436,24 +436,29 @@
     weights(0, w_gate, wn_gate, 'cols', 54)
     weights(1, w_up, wn_up, 'cols')
     services(56, 59)
-    weights = newton(O_Q, w_mid, scale_of(w_mid), 60)
-    weights(0, w_o, wn_o, 'rows')
+    newton(O_Q, w_mid, scale_of(w_mid), 60)
+    handed = [pltpu.make_async_copy(xbuf.at[:, pl.ds(0, w_mid)], own_out, wl_sem.at[0]),
+              pltpu.make_async_copy(xr.at[:, pl.ds(0, w_mid)], other_out, wl_sem.at[1])]
+    for copy in handed:
+        copy.start()
     services(70, PAIRS + 7)
-    weights(1, w_qkv, wn_qkv, 'groups')
     normalize(KEY_VALUE, 2 * GROUP_COLS, sb_ref)
-    copy = pltpu.make_async_copy(sb_ref, kv_out, kv_sem)
-    copy.start()
+    handed.append(pltpu.make_async_copy(sb_ref, kv_out, kv_sem))
+    handed[-1].start()
     for slot in range(4):
         for k in range(2):
             waited(mst.at[slot, k], ms_sem.at[slot, k])
-    copy.wait()
+    for copy in handed:
+        copy.wait()
 
 
 def main_step(grads, weights, moms):
     any_spec = pl.BlockSpec(memory_space=pl.ANY)
     ins = list(grads) + list(weights) + list(moms)
     d, width = weights[0].shape
-    outs = [jax.ShapeDtypeStruct(a.shape, F32) for a in list(weights) + list(moms)] + [jax.ShapeDtypeStruct((d, d), BF16)]
+    outs = [jax.ShapeDtypeStruct(a.shape, F32) for a in list(weights[2:]) + list(moms)] + [
+        jax.ShapeDtypeStruct((d, d), BF16), jax.ShapeDtypeStruct((d, weights[1].shape[0]), BF16),
+        jax.ShapeDtypeStruct((d, weights[1].shape[0]), F32)]
     w_long = weights[2].shape[1]
     dma = pltpu.SemaphoreType.DMA
     pieces = (PIECE_R, PIECE_C)
@@ -498,11 +503,11 @@
 
 
 def finish_kernel(*refs):
-    x_in, w_qkv = refs[:2]
-    srcs, out_far, dsts = refs[2:12], refs[12], refs[13:23]
-    x_ref, s_ref, sb_ref, t_ref, wk = refs[23:28]
-    bufs = refs[28:34]
-    in_sem, out_sem, wl_sem, ws_sem, x_sem = refs[34:]
+    x_in, own_in, other_in, w_qkv, w_o = refs[:5]
+    srcs, out_far, wn_qkv, wn_o, dsts = refs[5:13], refs[13], refs[14], refs[15], refs[16:24]
+    x_ref, x_own, s_ref, sb_ref, t_ref, wk = refs[24:30]
+    bufs = refs[30:36]
+    in_sem, out_sem, wl_sem, ws_sem, x_sem, step_sem, done_sem = refs[36:]
     d, w = out_far.shape
     load = pltpu.make_async_copy(x_in, x_ref, x_sem)
     load.start()
@@ -512,12 +517,21 @@
     for lo, at in heads:
         pltpu.make_async_copy(w_qkv.at[:, at], wk.at[:, lo:lo + HEAD_DIM], wl_sem).start()
 
-    moves = [(srcs[n], dsts[n]) for n in (4, 9, 2, 7, 3, 8)]
-    moves += [(srcs[n], dsts[n]) for n in (1, 6)]
-    moves += [(srcs[n].at[:, lo:lo + d], dsts[n].at[:, lo:lo + d]) for n in (0, 5) for lo in (0, d)]
+    square = [buf.at[:d, :d] for buf in bufs]
+    w_o_buf, w_q_buf, x_other = square[3:]
+    queries = [(slice(g * GROUP_COLS, (g + 1) * GROUP_COLS), slice(2 * g * GROUP_COLS, (2 * g + 1) * GROUP_COLS))
+               for g in range(d // GROUP_COLS)]
+    loads = [pltpu.make_async_copy(other_in, x_other, step_sem.at[0]), pltpu.make_async_copy(own_in, x_own, step_sem.at[1]),
+             pltpu.make_async_copy(w_o, w_o_buf, step_sem.at[2])]
+    for copy in loads:
+        copy.start()
+    for near, at in queries:
+        pltpu.make_async_copy(w_qkv.at[:, at], w_q_buf.at[:, near], step_sem.at[3]).start()
+    moves = [(srcs[n], dsts[n]) for n in (2, 7, 0, 5, 1, 6, 4)] + [(srcs[3].at[:, lo:lo + d], dsts[3].at[:, lo:lo + d]) for lo in (0, d)]
+    step_scale = 0.2 * math.sqrt(max(d, 2 * x_own.shape[1]))
 
     def held(n):
-        return bufs[n] if n < 6 else bufs[n - 6].at[:d, :d]
+        return bufs[n] if n < 6 else square[n - 6]
 
     def fetch(n):
         if n >= 6:
@@ -531,11 +545,42 @@
         pltpu.make_async_copy(moves[n][0], held(n), in_sem.at[n]).wait()
         put_copy(n).start()
 
-    for n in range(6):
+    def panels(mine, one):
+        def loop(read):
+            def body(c, carry):
+                cols = ds(c * GROUP_COLS, GROUP_COLS)
+                one(cols, read(cols))
+                return carry
+            lax.fori_loop(0, d // GROUP_COLS, body, 0)
+        pl.when(core == mine)(lambda: loop(lambda cols: x_own[:, cols].astype(F32)))
+        pl.when(core != mine)(lambda: loop(lambda cols: x_other[:, cols]))
+
+    def step_o(unused):
+        for copy in loads:
+            copy.wait()
+
+        def one(rows, x_orth):
+            w_o_buf[rows, :] = weight_step(w_o_buf[rows, :], x_orth.T, step_scale)
+        panels(0, one)
+        pltpu.make_async_copy(w_o_buf, wn_o, done_sem.at[0]).start()
+
+    def step_q(unused):
+        pltpu.make_async_copy(w_q_buf, w_q_buf, step_sem.at[3]).wait()
+
+        def one(cols, x_orth):
+            w_q_buf[:, cols] = weight_step(w_q_buf[:, cols], x_orth, step_scale)
+        panels(1, one)
+        for near, at in queries:
+            pltpu.make_async_copy(w_q_buf.at[:, near], wn_qkv.at[:, at], done_sem.at[1]).start()
+
+    def freed(which):
+        pltpu.make_async_copy((w_o_buf, w_q_buf)[which], (w_o_buf, w_q_buf)[which], done_sem.at[which]).wait()
+
+    for n in range(3):
         fetch(n)
-    plan = {(0, 1): ((put, 0),), (0, 2): ((put, 1),), (1, 0): ((put, 2),), (1, 1): ((put, 3),), (1, 2): ((fetch, 6),),
-            (2, 0): ((put, 4),), (2, 1): ((put, 5), (fetch, 7)), (2, 2): ((fetch, 8),), (3, 0): ((put, 6), (fetch, 9)),
-            (3, 1): ((put, 7), (fetch, 10)), (3, 2): ((put, 8),), (4, 0): ((fetch, 11), (put, 9)), (4, 1): ((put, 10),)}
+    plan = {(0, 2): ((step_o, 0), (put, 0)), (1, 0): ((step_q, 0), (put, 1), (fetch, 5)), (1, 1): ((put, 2),),
+            (1, 2): ((freed, 0), (fetch, 3)), (2, 0): ((freed, 1), (fetch, 4), (fetch, 6)), (2, 1): ((put, 5), (fetch, 7)),
+            (2, 2): ((put, 3), (fetch, 8)), (3, 0): ((put, 4),), (3, 1): ((put, 6),), (3, 2): ((put, 7),), (4, 0): ((put, 8),)}
 
     def step(i, carry):
         def at(slot):
@@ -563,7 +608,6 @@
 
     load.wait()
     lax.fori_loop(0, NEWTON_STEPS, step, 0)
-    put(11)
     for c in range(w // PANEL):
         cols = slice(c * PANEL, (c + 1) * PANEL)
         out_far[:, cols] = advanced(t_ref, x_ref, pl.ds(w + c * PANEL, PANEL)).astype(F32)
@@ -571,29 +615,33 @@
     for c in range(w // PANEL):
         cols = slice(c * PANEL, (c + 1) * PANEL)
         wk[:, cols] = weight_step(wk[:, cols], advanced(t_ref, x_ref, pl.ds(c * PANEL, PANEL)).astype(F32), scale)
-    for n in range(6, 12):
+    for lo, at in heads:
+        pltpu.make_async_copy(wk.at[:, lo:lo + HEAD_DIM], wn_qkv.at[:, at], ws_sem).start()
+    for n in range(3, 9):
         put_copy(n).wait()
-    for lo, at in heads:
-        pltpu.make_async_copy(wk.at[:, lo:lo + HEAD_DIM], dsts[0].at[:, at], ws_sem).start()
     pltpu.make_async_copy(wk, wk, ws_sem).wait()
 
 
-def finish(x_kv, w_qkv, arrays):
-    d = x_kv.shape[0]
-    w = x_kv.shape[1] // 2
+def finish(handed, w_qkv, w_o, arrays):
+    d = handed[0].shape[0]
+    w = handed[0].shape[1] // 2
+    ins = list(handed) + [w_qkv, w_o] + list(arrays)
     any_spec = pl.BlockSpec(memory_space=pl.ANY)
     vmem = pl.BlockSpec(memory_space=pltpu.VMEM)
     dma = pltpu.SemaphoreType.DMA
+    outs = [jax.ShapeDtypeStruct((d, w), F32)] + [jax.ShapeDtypeStruct(a.shape, F32) for a in [w_qkv, w_o] + list(arrays)]
     return pl.pallas_call(
         finish_kernel,
-        out_shape=[jax.ShapeDtypeStruct((d, w), F32)] + [jax.ShapeDtypeStruct(a.shape, F32) for a in arrays],
-        in_specs=[any_spec] * (len(arrays) + 2),
-        out_specs=[vmem] + [any_spec] * len(arrays),
-        scratch_shapes=[pltpu.VMEM((d, d), BF16), pltpu.VMEM((d, d), F32), pltpu.VMEM((d, d), BF16), pltpu.VMEM((d, d), BF16), pltpu.VMEM((d, w), F32)]
-        + [pltpu.VMEM(arrays[n].shape, F32) for n in (4, 9, 2, 7, 3, 8)] + [dma((12,)), dma((12,)), dma, dma, dma],
+        out_shape=outs,
+        in_specs=[any_spec] * len(ins),
+        out_specs=[vmem] + [any_spec] * (len(outs) - 1),
+        scratch_shapes=[pltpu.VMEM((d, d), BF16), pltpu.VMEM(handed[1].shape, BF16), pltpu.VMEM((d, d), F32), pltpu.VMEM((d, d), BF16),
+                        pltpu.VMEM((d, d), BF16), pltpu.VMEM((d, w), F32)]
+        + [pltpu.VMEM(arrays[n].shape, F32) for n in (2, 7, 0, 5, 1, 6)]
+        + [dma((9,)), dma((9,)), dma, dma, dma, dma((4,)), dma((2,))],
         compiler_params=pltpu.CompilerParams(vmem_limit_bytes=VMEM_BYTES),
         cost_estimate=pl.CostEstimate(flops=3 * 10 ** 10, bytes_accessed=12 * 10 ** 7, transcendentals=0),
-    )(x_kv, w_qkv, *arrays)
+    )(*ins)
 
 
 def solution(mesh):
@@ -610,7 +658,7 @@
     def local_step(*arrays):
         weights, moms = arrays[5:10], arrays[10:]
         results = main_step([block[0] for block in arrays[:5]], weights, moms)
-        done = finish(results[10], weights[0], results[:10])
+        done = finish(results[8:], weights[0], weights[1], results[:8])
         x_far, done = done[0], list(done[1:])
         scale = 0.2 * math.sqrt(max(x_far.shape[0], x_far.shape[1] * tp_count))
         core = lax.axis_index('tp').astype(jnp.int32).reshape(1)

time: 604 us -> 601 us (level)
    pallas_call x1, Pallas kernels: 547 us -> 538 us  [main_step(): pl.pallas_call(step_kernel, out_shape=outs, in_specs=[any_spec] * len(ins...]
where the time goes in v4:
time: 601 us; the launch traced here: 600 us
  Pallas kernels  595 us (99%)
    pallas_call x1, Pallas kernels, main_step(): pl.pallas_call(step_kernel, out_shape=outs, in_specs=[any_spec] * len(ins...  538 us
    pallas_call x1, Pallas kernels, finish(): pl.pallas_call(finish_kernel, out_shape=outs, in_specs=[any_spec] * len(i...  52.6 us
  transfers between devices with their start and end apart: 1, of which 1 were waited for; matrix products, arithmetic and copies ran while one was open for 0% of the time, Pallas kernels for 0%

profile of v4, /device:TPU:0, one launch (start us, length us, event | category | flops | bytes accessed | tf_op | source)
XLA Modules:
  0.0 600.1 jit_solution(7394251498596058996)
XLA Ops:
  0.6 538.1 %shard_map.222 = (f32[1024,1536]{1,0:T(8,128)}, f32[1024,1536]{1,0:T(8,128)}, f32[1536,1024]{1,0:T(8,128)}, f32[1024,2048]{1,0:T(8,128)}, f32[1024,1024]{1,0:T(8...) custom-call(bf16[1024,2048]{1,0:T(8,128)(2,1)} %bitcast.6, ...), custom_call_target="tpu_custom_call" | custom-call | flops 99999997952 | bytes 200000000 | tf_op jit(solution)/shard_map/pallas_call | solution.py:465
  538.8 52.6 %shard_map.223 = (f32[1024,512]{1,0:T(8,128)}, f32[1024,2048]{1,0:T(8,128)}, f32[1024,1024]{1,0:T(8,128)}, f32[1024,1536]{1,0:T(8,128)}, f32[1024,1536]{1,0:T(8,...) custom-call(bf16[1024,1024]{1,0:T(8,128)(2,1)} %get-tuple-element.32, ...), custom_call_target="tpu_custom_call" | custom-call | flops 30000001024 | bytes 120000000 | tf_op jit(solution)/shard_map/pallas_call | solution.py:633
  591.4 0.6 collective-permute-start
  592.0 3.8 collective-permute-done.back_ref
  595.8 4.3 shard_map.224
Async XLA Ops:
  591.4 4.4 collective-permute-start

commit v5 on v4

--- a/solution.py
+++ b/solution.py
@@ -29,7 +29,7 @@
 HALF_R = PIECE_R // 2
 QUART_R = PIECE_R // 4
 DOWN, GATE_UP, O_Q, KEY_VALUE = range(4)
-KV_DELAY = 5
+KV_DELAY = 4
 FIRST = (0, 12, 36, 52 + KV_DELAY)
 LAST = (12, 36, 52, 60 + KV_DELAY)
 PAIRS = LAST[-1]
@@ -521,29 +521,32 @@
     w_o_buf, w_q_buf, x_other = square[3:]
     queries = [(slice(g * GROUP_COLS, (g + 1) * GROUP_COLS), slice(2 * g * GROUP_COLS, (2 * g + 1) * GROUP_COLS))
                for g in range(d // GROUP_COLS)]
+    moves = [(srcs[n], dsts[n]) for n in (2, 7, 0, 5, 1, 6, 4)] + [(srcs[3].at[:, lo:lo + d], dsts[3].at[:, lo:lo + d]) for lo in (0, d)]
+    step_scale = 0.2 * math.sqrt(max(d, 2 * x_own.shape[1]))
+
+    def held(n):
+        return bufs[n] if n < 6 else square[n - 6]
+
+    def fetch(n):
+        if n >= 6:
+            put_copy(n - 6).wait()
+        pltpu.make_async_copy(moves[n][0], held(n), in_sem.at[n]).start()
+
+    def put_copy(n):
+        return pltpu.make_async_copy(held(n), moves[n][1], out_sem.at[n])
+
+    def put(n):
+        pltpu.make_async_copy(moves[n][0], held(n), in_sem.at[n]).wait()
+        put_copy(n).start()
+
+    for n in range(3):
+        fetch(n)
     loads = [pltpu.make_async_copy(other_in, x_other, step_sem.at[0]), pltpu.make_async_copy(own_in, x_own, step_sem.at[1]),
              pltpu.make_async_copy(w_o, w_o_buf, step_sem.at[2])]
     for copy in loads:
         copy.start()
     for near, at in queries:
         pltpu.make_async_copy(w_qkv.at[:, at], w_q_buf.at[:, near], step_sem.at[3]).start()
-    moves = [(srcs[n], dsts[n]) for n in (2, 7, 0, 5, 1, 6, 4)] + [(srcs[3].at[:, lo:lo + d], dsts[3].at[:, lo:lo + d]) for lo in (0, d)]
-    step_scale = 0.2 * math.sqrt(max(d, 2 * x_own.shape[1]))
-
-    def held(n):
-        return bufs[n] if n < 6 else square[n - 6]
-
-    def fetch(n):
-        if n >= 6:
-            put_copy(n - 6).wait()
-        pltpu.make_async_copy(moves[n][0], held(n), in_sem.at[n]).start()
-
-    def put_copy(n):
-        return pltpu.make_async_copy(held(n), moves[n][1], out_sem.at[n])
-
-    def put(n):
-        pltpu.make_async_copy(moves[n][0], held(n), in_sem.at[n]).wait()
-        put_copy(n).start()
 
     def panels(mine, one):
         def loop(read):
@@ -576,11 +579,9 @@
     def freed(which):
         pltpu.make_async_copy((w_o_buf, w_q_buf)[which], (w_o_buf, w_q_buf)[which], done_sem.at[which]).wait()
 
-    for n in range(3):
-        fetch(n)
-    plan = {(0, 2): ((step_o, 0), (put, 0)), (1, 0): ((step_q, 0), (put, 1), (fetch, 5)), (1, 1): ((put, 2),),
-            (1, 2): ((freed, 0), (fetch, 3)), (2, 0): ((freed, 1), (fetch, 4), (fetch, 6)), (2, 1): ((put, 5), (fetch, 7)),
-            (2, 2): ((put, 3), (fetch, 8)), (3, 0): ((put, 4),), (3, 1): ((put, 6),), (3, 2): ((put, 7),), (4, 0): ((put, 8),)}
+    plan = {(0, 1): ((put, 0),), (0, 2): ((put, 1),), (1, 0): ((put, 2), (fetch, 6)), (1, 1): ((step_o, 0), (fetch, 7)),
+            (1, 2): ((step_q, 0), (fetch, 5), (fetch, 8)), (2, 0): ((freed, 0), (fetch, 3), (freed, 1), (fetch, 4), (put, 6)),
+            (2, 1): ((put, 7),), (2, 2): ((put, 5),), (3, 0): ((put, 8),), (3, 1): ((put, 3),), (3, 2): ((put, 4),)}
 
     def step(i, carry):
         def at(slot):

time: 601 us -> 597 us (level)
  no operation moved by 1% of the time
where the time goes in v5:
time: 597 us
  Pallas kernels  592 us (99%)
    pallas_call x1, Pallas kernels, main_step(): pl.pallas_call(step_kernel, out_shape=outs, in_specs=[any_spec] * len(ins...  536 us
    pallas_call x1, Pallas kernels, finish(): pl.pallas_call(finish_kernel, out_shape=outs, in_specs=[any_spec] * len(i...  51.3 us
  transfers between devices with their start and end apart: 1, of which 1 were waited for; matrix products, arithmetic and copies ran while one was open for 0% of the time, Pallas kernels for 0%

profile of v5, /device:TPU:0, one launch (start us, length us, event | category | flops | bytes accessed | tf_op | source)
XLA Modules:
  0.0 596.7 jit_solution(13620043457071395566)
XLA Ops:
  0.6 536.4 %shard_map.222 = (f32[1024,1536]{1,0:T(8,128)}, f32[1024,1536]{1,0:T(8,128)}, f32[1536,1024]{1,0:T(8,128)}, f32[1024,2048]{1,0:T(8,128)}, f32[1024,1024]{1,0:T(8...) custom-call(bf16[1024,2048]{1,0:T(8,128)(2,1)} %bitcast.6, ...), custom_call_target="tpu_custom_call" | custom-call | flops 99999997952 | bytes 200000000 | tf_op jit(solution)/shard_map/pallas_call | solution.py:465
  537.0 51.3 %shard_map.223 = (f32[1024,512]{1,0:T(8,128)}, f32[1024,2048]{1,0:T(8,128)}, f32[1024,1024]{1,0:T(8,128)}, f32[1024,1536]{1,0:T(8,128)}, f32[1024,1536]{1,0:T(8,...) custom-call(bf16[1024,1024]{1,0:T(8,128)(2,1)} %get-tuple-element.32, ...), custom_call_target="tpu_custom_call" | custom-call | flops 30000001024 | bytes 120000000 | tf_op jit(solution)/shard_map/pallas_call | solution.py:634
  588.3 0.2 collective-permute-start
  588.5 3.9 collective-permute-done.back_ref
  592.4 4.3 shard_map.224
Async XLA Ops:
  588.3 4.1 collective-permute-start

commit v6 on v5

--- a/solution.py
+++ b/solution.py
@@ -579,9 +579,10 @@
     def freed(which):
         pltpu.make_async_copy((w_o_buf, w_q_buf)[which], (w_o_buf, w_q_buf)[which], done_sem.at[which]).wait()
 
-    plan = {(0, 1): ((put, 0),), (0, 2): ((put, 1),), (1, 0): ((put, 2), (fetch, 6)), (1, 1): ((step_o, 0), (fetch, 7)),
-            (1, 2): ((step_q, 0), (fetch, 5), (fetch, 8)), (2, 0): ((freed, 0), (fetch, 3), (freed, 1), (fetch, 4), (put, 6)),
-            (2, 1): ((put, 7),), (2, 2): ((put, 5),), (3, 0): ((put, 8),), (3, 1): ((put, 3),), (3, 2): ((put, 4),)}
+    plan = {(0, 1): ((put, 0),), (0, 2): ((put, 1),), (1, 0): ((put, 2), (fetch, 6)), (1, 1): ((fetch, 7),),
+            (1, 2): ((put, 6), (fetch, 8)), (2, 0): ((put, 7), (step_o, 0)), (2, 1): ((step_q, 0), (fetch, 5), (put, 8)),
+            (2, 2): ((freed, 0), (fetch, 3)), (3, 0): ((freed, 1), (fetch, 4)), (3, 1): ((put, 5),), (3, 2): ((put, 3),),
+            (4, 0): ((put, 4),)}
 
     def step(i, carry):
         def at(slot):

time: 597 us -> 596 us (level)
  no operation moved by 1% of the time
where the time goes in v6:
time: 596 us
  Pallas kernels  591 us (99%)
    pallas_call x1, Pallas kernels, main_step(): pl.pallas_call(step_kernel, out_shape=outs, in_specs=[any_spec] * len(ins...  536 us
    pallas_call x1, Pallas kernels, finish(): pl.pallas_call(finish_kernel, out_shape=outs, in_specs=[any_spec] * len(i...  50.1 us
  transfers between devices with their start and end apart: 1, of which 1 were waited for; matrix products, arithmetic and copies ran while one was open for 0% of the time, Pallas kernels for 0%

profile of v6, /device:TPU:0, one launch (start us, length us, event | category | flops | bytes accessed | tf_op | source)
XLA Modules:
  0.0 595.6 jit_solution(13219144360008277730)
XLA Ops:
  0.6 536.4 %shard_map.222 = (f32[1024,1536]{1,0:T(8,128)}, f32[1024,1536]{1,0:T(8,128)}, f32[1536,1024]{1,0:T(8,128)}, f32[1024,2048]{1,0:T(8,128)}, f32[1024,1024]{1,0:T(8...) custom-call(bf16[1024,2048]{1,0:T(8,128)(2,1)} %bitcast.6, ...), custom_call_target="tpu_custom_call" | custom-call | flops 99999997952 | bytes 200000000 | tf_op jit(solution)/shard_map/pallas_call | solution.py:465
  537.0 50.1 %shard_map.223 = (f32[1024,512]{1,0:T(8,128)}, f32[1024,2048]{1,0:T(8,128)}, f32[1024,1024]{1,0:T(8,128)}, f32[1024,1536]{1,0:T(8,128)}, f32[1024,1536]{1,0:T(8,...) custom-call(bf16[1024,1024]{1,0:T(8,128)(2,1)} %get-tuple-element.32, ...), custom_call_target="tpu_custom_call" | custom-call | flops 30000001024 | bytes 120000000 | tf_op jit(solution)/shard_map/pallas_call | solution.py:635
  587.2 0.4 collective-permute-start
  587.5 3.8 collective-permute-done.back_ref
  591.3 4.3 shard_map.224
Async XLA Ops:
  587.2 4.2 collective-permute-start
